TPU v7x, 32 devices: a 4x4x1 block of a 4x4x8 slice. The times are simulated.
32 devices in a mesh: dp: 1 (over z), tp: 4 (over y), pp: 8 (over x, core).
Axes of the slice: x: 4, y: 4, z: 1, core: 2. Of those that a mesh axis runs over, the one named last changes fastest.
The devices are a block of a 4x4x8 slice.
Arguments:
- x_in: bfloat16 [2, 6, 256, 2048], P(None, 'dp', 'tp')
- ln_params: float32 [8, 4, 2048], P('pp')
- w_q: bfloat16 [8, 2048, 16, 1, 128], P('pp', None, 'tp')
- w_k: bfloat16 [8, 2048, 16, 128], P('pp', None, 'tp')
- w_v: bfloat16 [8, 2048, 16, 128], P('pp', None, 'tp')
- w_o: bfloat16 [8, 16, 1, 128, 2048], P('pp', 'tp')
- w_up: bfloat16 [8, 2048, 8192], P('pp', None, 'tp')
- w_down: bfloat16 [8, 8192, 2048], P('pp', 'tp')
Outputs:
- output: bfloat16 [8, 2, 6, 256, 2048], P('pp', None, 'dp', 'tp')
All inputs are finite; a program needn't handle non-finite values.
Results may differ from a plain program's by a relative error of at most 0.0196532.
Values are sent between devices in bfloat16 or wider.
A program may use at most 768 MiB of HBM per device.

v0:
```python
import jax
import jax.numpy as jnp
from jax import lax
from jax.sharding import PartitionSpec as P

LN_EPS = 1e-5
ROPE_BASE = 10000.0


def layer_norm(x_act, ln_gain, ln_bias):
    x_f32 = x_act.astype(jnp.float32)
    row_mean = jnp.mean(x_f32, axis=-1, keepdims=True)
    centred = x_f32 - row_mean
    variance = jnp.mean(centred * centred, axis=-1, keepdims=True)
    return (centred * lax.rsqrt(variance + LN_EPS) * ln_gain + ln_bias).astype(jnp.bfloat16)


def rope_tables(seq_len, head_dim):
    positions = jnp.arange(seq_len, dtype=jnp.float32)
    inv_freq = ROPE_BASE ** (-2.0 * jnp.arange(head_dim // 2, dtype=jnp.float32) / head_dim)
    angles = positions[:, None] * inv_freq[None, :]
    return jnp.cos(angles), jnp.sin(angles)


def apply_rope(proj, cos_tab, sin_tab):
    half_dim = proj.shape[-1] // 2
    table_shape = (1, proj.shape[1]) + (1,) * (proj.ndim - 3) + (half_dim,)
    cos_bcast = cos_tab.reshape(table_shape)
    sin_bcast = sin_tab.reshape(table_shape)
    first_half = proj[..., :half_dim]
    second_half = proj[..., half_dim:]
    return jnp.concatenate([first_half * cos_bcast - second_half * sin_bcast, second_half * cos_bcast + first_half * sin_bcast], axis=-1)


def causal_attention(q_proj, k_proj, v_proj):
    seq_len = q_proj.shape[1]
    scores = jnp.einsum("btkgh,bskh->bktgs", q_proj, k_proj, preferred_element_type=jnp.float32) * (q_proj.shape[-1] ** -0.5)
    positions = jnp.arange(seq_len)
    allowed = positions[:, None, None] >= positions[None, None, :]
    probs_bf = jax.nn.softmax(jnp.where(allowed, scores, -1e30), axis=-1).astype(jnp.bfloat16)
    return jnp.einsum("bktgs,bskh->bktgh", probs_bf, v_proj, preferred_element_type=jnp.float32).astype(jnp.bfloat16)


def branch_partial(x_full, ln_par, w_q, w_k, w_v, w_o, w_up, w_down):
    batch_dim, seq_len, d_model = x_full.shape
    kv_local, group_size, head_dim = w_q.shape[1:]
    num_rows = batch_dim * seq_len
    h_attn = layer_norm(x_full, ln_par[0], ln_par[1]).reshape(num_rows, d_model)
    h_mlp = layer_norm(x_full, ln_par[2], ln_par[3]).reshape(num_rows, d_model)
    cos_tab, sin_tab = rope_tables(seq_len, head_dim)
    q_proj = jnp.dot(h_attn, w_q.reshape(d_model, -1), preferred_element_type=jnp.float32)
    q_proj = apply_rope(q_proj.reshape(batch_dim, seq_len, kv_local, group_size, head_dim), cos_tab, sin_tab).astype(jnp.bfloat16)
    k_proj = jnp.dot(h_attn, w_k.reshape(d_model, -1), preferred_element_type=jnp.float32)
    k_proj = apply_rope(k_proj.reshape(batch_dim, seq_len, kv_local, head_dim), cos_tab, sin_tab).astype(jnp.bfloat16)
    v_proj = jnp.dot(h_attn, w_v.reshape(d_model, -1), preferred_element_type=jnp.float32).astype(jnp.bfloat16)
    v_proj = v_proj.reshape(batch_dim, seq_len, kv_local, head_dim)
    context = causal_attention(q_proj, k_proj, v_proj)
    attn_out = jnp.einsum("bktgh,kghd->btd", context, w_o, preferred_element_type=jnp.float32)
    hidden = jax.nn.gelu(jnp.dot(h_mlp, w_up, preferred_element_type=jnp.float32), approximate=False).astype(jnp.bfloat16)
    mlp_out = jnp.dot(hidden, w_down, preferred_element_type=jnp.float32).reshape(batch_dim, seq_len, d_model)
    return (attn_out + mlp_out).astype(jnp.bfloat16)


def solution(mesh):
    pp_size = mesh.shape["pp"]
    send_pairs = [(src_idx, src_idx + 1) for src_idx in range(pp_size - 1)]

    def stage_layer(x_shard, layer_weights):
        ln_par, wq_s, wk_s, wv_s, wo_s, wup_s, wdown_s = layer_weights
        x_full = lax.all_gather(x_shard, "tp", axis=1, tiled=True)
        partial_sum = branch_partial(x_full, ln_par, wq_s, wk_s, wv_s, wo_s, wup_s, wdown_s)
        reduced = lax.psum_scatter(partial_sum, "tp", scatter_dimension=1, tiled=True)
        return (x_shard.astype(jnp.float32) + reduced.astype(jnp.float32)).astype(jnp.bfloat16)

    def stage_body(x_in, ln_params, w_q, w_k, w_v, w_o, w_up, w_down):
        stage_idx = lax.axis_index("pp")
        num_micro = x_in.shape[0]
        layer_weights = (ln_params[0], w_q[0], w_k[0], w_v[0], w_o[0], w_up[0], w_down[0])

        def micro_step(step_idx, loop_carry):
            recv_buf, out_buf = loop_carry
            first_in = lax.dynamic_index_in_dim(x_in, jnp.minimum(step_idx, num_micro - 1), axis=0, keepdims=False)
            layer_in = jnp.where(stage_idx == 0, first_in, recv_buf)
            layer_out = stage_layer(layer_in, layer_weights)
            slot_idx = step_idx - stage_idx
            is_valid = (slot_idx >= 0) & (slot_idx < num_micro)
            slot_safe = jnp.clip(slot_idx, 0, num_micro - 1)
            previous = lax.dynamic_index_in_dim(out_buf, slot_safe, axis=0, keepdims=False)
            out_buf = lax.dynamic_update_index_in_dim(out_buf, jnp.where(is_valid, layer_out, previous), slot_safe, axis=0)
            recv_buf = lax.ppermute(layer_out, "pp", send_pairs)
            return recv_buf, out_buf

        init_carry = (jnp.zeros_like(x_in[0]), jnp.zeros_like(x_in))
        _, out_buf = lax.fori_loop(0, num_micro + pp_size - 1, micro_step, init_carry)
        return out_buf[None]

    in_specs = (P(None, "dp", "tp", None), P("pp", None, None), P("pp", None, "tp", None, None), P("pp", None, "tp", None), P("pp", None, "tp", None), P("pp", "tp", None, None, None), P("pp", None, "tp"), P("pp", "tp", None))
    return jax.shard_map(stage_body, mesh=mesh, in_specs=in_specs, out_specs=P("pp", None, "dp", "tp", None), check_vma=False)
```

profile of v0, /device:TPU:119, one launch (start us, length us, event | category | flops | bytes accessed | tf_op | source)
XLA Modules:
  0.0 2419.8 jit_solution(18087112463457225487)
XLA Ops:
  17.4 2395.5 %while.17 = (s32[]{:T(128)}, bf16[6,64,2048]{2,1,0:T(8,128)(2,1)S(1)}, bf16[2,6,64,2048]{3,2,1,0:T(8,128)(2,1)}, pred[]{:T(512)}, bf16[2,6,64,2048]{3,2,1,0:T(8,...) while((s32[]{:T(128)}, ...), condition=%wide.region_6.7_spmd, body=%wide.region_0.6_spmd.sunk | while | flops 39757373440 | bytes 433069376 | solution.py:94
  22.3 61.9 %all-gather.2.cloned.1.call-done = bf16[6,256,2048]{2,1,0:T(8,128)(2,1)} async-done(((bf16[6,64,2048]{2,1,0:T(8,128)(2,1)}), bf16[6,256,2048]{2,1,0:T(8,128)(2,1)}) %all-gather.2.cloned.1.call-update) | async-done | bytes 6291472 | tf_op jit(solution)/shard_map/while/body/eval_jaxpr/all_gather | solution.py:70
  119.0 41.5 %fusion.159 = bf16[1536,2048]{1,0:T(8,128)(2,1)} fusion(bf16[1536,2048]{1,0:T(8,128)(2,1)S(1)} %bitcast.133, bf16[2048,2048]{1,0:T(8,128)(2,1)S(1)} %bitcast.143), kind=kOutput, calls=%fused_computation.15.clone.clone.1.clone.1 | convolution fusion | flops 13089374208 | bytes 20971520 | tf_op jit(solution)/shard_map/while/body/eval_jaxpr/dot_general | solution.py:59
  199.8 59.7 %reduce-scatter.2.cloned.1.call-done = bf16[6,64,2048]{2,1,0:T(8,128)(2,1)} async-done(((bf16[6,256,2048]{2,1,0:T(8,128)(2,1)}), bf16[6,64,2048]{2,1,0:T(8,128)(2,1)}) %reduce-scatter.2.cloned.1.call-update) | async-done | bytes 1572880 | tf_op jit(solution)/shard_map/while/body/eval_jaxpr/reduce_scatter | solution.py:72
  274.1 78.0 %all-gather.2.cloned.1.call-done = bf16[6,256,2048]{2,1,0:T(8,128)(2,1)} async-done(((bf16[6,64,2048]{2,1,0:T(8,128)(2,1)}), bf16[6,256,2048]{2,1,0:T(8,128)(2,1)}) %all-gather.2.cloned.1.call-update) | async-done | bytes 6291472 | tf_op jit(solution)/shard_map/while/body/eval_jaxpr/all_gather | solution.py:70
  386.9 41.5 %fusion.159 = bf16[1536,2048]{1,0:T(8,128)(2,1)} fusion(bf16[1536,2048]{1,0:T(8,128)(2,1)S(1)} %bitcast.133, bf16[2048,2048]{1,0:T(8,128)(2,1)S(1)} %bitcast.143), kind=kOutput, calls=%fused_computation.15.clone.clone.1.clone.1 | convolution fusion | flops 13089374208 | bytes 20971520 | tf_op jit(solution)/shard_map/while/body/eval_jaxpr/dot_general | solution.py:59
  434.3 17.5 fusion.160
  467.7 59.7 %reduce-scatter.2.cloned.1.call-done = bf16[6,64,2048]{2,1,0:T(8,128)(2,1)} async-done(((bf16[6,256,2048]{2,1,0:T(8,128)(2,1)}), bf16[6,64,2048]{2,1,0:T(8,128)(2,1)}) %reduce-scatter.2.cloned.1.call-update) | async-done | bytes 1572880 | tf_op jit(solution)/shard_map/while/body/eval_jaxpr/reduce_scatter | solution.py:72
  542.0 78.0 %all-gather.2.cloned.1.call-done = bf16[6,256,2048]{2,1,0:T(8,128)(2,1)} async-done(((bf16[6,64,2048]{2,1,0:T(8,128)(2,1)}), bf16[6,256,2048]{2,1,0:T(8,128)(2,1)}) %all-gather.2.cloned.1.call-update) | async-done | bytes 6291472 | tf_op jit(solution)/shard_map/while/body/eval_jaxpr/all_gather | solution.py:70
  654.9 41.5 %fusion.159 = bf16[1536,2048]{1,0:T(8,128)(2,1)} fusion(bf16[1536,2048]{1,0:T(8,128)(2,1)S(1)} %bitcast.133, bf16[2048,2048]{1,0:T(8,128)(2,1)S(1)} %bitcast.143), kind=kOutput, calls=%fused_computation.15.clone.clone.1.clone.1 | convolution fusion | flops 13089374208 | bytes 20971520 | tf_op jit(solution)/shard_map/while/body/eval_jaxpr/dot_general | solution.py:59
  735.7 59.7 %reduce-scatter.2.cloned.1.call-done = bf16[6,64,2048]{2,1,0:T(8,128)(2,1)} async-done(((bf16[6,256,2048]{2,1,0:T(8,128)(2,1)}), bf16[6,64,2048]{2,1,0:T(8,128)(2,1)}) %reduce-scatter.2.cloned.1.call-update) | async-done | bytes 1572880 | tf_op jit(solution)/shard_map/while/body/eval_jaxpr/reduce_scatter | solution.py:72
  810.0 78.0 %all-gather.2.cloned.1.call-done = bf16[6,256,2048]{2,1,0:T(8,128)(2,1)} async-done(((bf16[6,64,2048]{2,1,0:T(8,128)(2,1)}), bf16[6,256,2048]{2,1,0:T(8,128)(2,1)}) %all-gather.2.cloned.1.call-update) | async-done | bytes 6291472 | tf_op jit(solution)/shard_map/while/body/eval_jaxpr/all_gather | solution.py:70
  922.8 41.5 %fusion.159 = bf16[1536,2048]{1,0:T(8,128)(2,1)} fusion(bf16[1536,2048]{1,0:T(8,128)(2,1)S(1)} %bitcast.133, bf16[2048,2048]{1,0:T(8,128)(2,1)S(1)} %bitcast.143), kind=kOutput, calls=%fused_computation.15.clone.clone.1.clone.1 | convolution fusion | flops 13089374208 | bytes 20971520 | tf_op jit(solution)/shard_map/while/body/eval_jaxpr/dot_general | solution.py:59
  1003.6 59.7 %reduce-scatter.2.cloned.1.call-done = bf16[6,64,2048]{2,1,0:T(8,128)(2,1)} async-done(((bf16[6,256,2048]{2,1,0:T(8,128)(2,1)}), bf16[6,64,2048]{2,1,0:T(8,128)(2,1)}) %reduce-scatter.2.cloned.1.call-update) | async-done | bytes 1572880 | tf_op jit(solution)/shard_map/while/body/eval_jaxpr/reduce_scatter | solution.py:72
  1078.0 78.0 %all-gather.2.cloned.1.call-done = bf16[6,256,2048]{2,1,0:T(8,128)(2,1)} async-done(((bf16[6,64,2048]{2,1,0:T(8,128)(2,1)}), bf16[6,256,2048]{2,1,0:T(8,128)(2,1)}) %all-gather.2.cloned.1.call-update) | async-done | bytes 6291472 | tf_op jit(solution)/shard_map/while/body/eval_jaxpr/all_gather | solution.py:70
  1190.8 41.5 %fusion.159 = bf16[1536,2048]{1,0:T(8,128)(2,1)} fusion(bf16[1536,2048]{1,0:T(8,128)(2,1)S(1)} %bitcast.133, bf16[2048,2048]{1,0:T(8,128)(2,1)S(1)} %bitcast.143), kind=kOutput, calls=%fused_computation.15.clone.clone.1.clone.1 | convolution fusion | flops 13089374208 | bytes 20971520 | tf_op jit(solution)/shard_map/while/body/eval_jaxpr/dot_general | solution.py:59
  1238.2 17.5 fusion.160
  1271.6 59.7 %reduce-scatter.2.cloned.1.call-done = bf16[6,64,2048]{2,1,0:T(8,128)(2,1)} async-done(((bf16[6,256,2048]{2,1,0:T(8,128)(2,1)}), bf16[6,64,2048]{2,1,0:T(8,128)(2,1)}) %reduce-scatter.2.cloned.1.call-update) | async-done | bytes 1572880 | tf_op jit(solution)/shard_map/while/body/eval_jaxpr/reduce_scatter | solution.py:72
  1345.9 78.0 %all-gather.2.cloned.1.call-done = bf16[6,256,2048]{2,1,0:T(8,128)(2,1)} async-done(((bf16[6,64,2048]{2,1,0:T(8,128)(2,1)}), bf16[6,256,2048]{2,1,0:T(8,128)(2,1)}) %all-gather.2.cloned.1.call-update) | async-done | bytes 6291472 | tf_op jit(solution)/shard_map/while/body/eval_jaxpr/all_gather | solution.py:70
  1458.8 41.5 %fusion.159 = bf16[1536,2048]{1,0:T(8,128)(2,1)} fusion(bf16[1536,2048]{1,0:T(8,128)(2,1)S(1)} %bitcast.133, bf16[2048,2048]{1,0:T(8,128)(2,1)S(1)} %bitcast.143), kind=kOutput, calls=%fused_computation.15.clone.clone.1.clone.1 | convolution fusion | flops 13089374208 | bytes 20971520 | tf_op jit(solution)/shard_map/while/body/eval_jaxpr/dot_general | solution.py:59
  1506.1 17.5 fusion.160
  1539.5 59.7 %reduce-scatter.2.cloned.1.call-done = bf16[6,64,2048]{2,1,0:T(8,128)(2,1)} async-done(((bf16[6,256,2048]{2,1,0:T(8,128)(2,1)}), bf16[6,64,2048]{2,1,0:T(8,128)(2,1)}) %reduce-scatter.2.cloned.1.call-update) | async-done | bytes 1572880 | tf_op jit(solution)/shard_map/while/body/eval_jaxpr/reduce_scatter | solution.py:72
  1613.9 78.0 %all-gather.2.cloned.1.call-done = bf16[6,256,2048]{2,1,0:T(8,128)(2,1)} async-done(((bf16[6,64,2048]{2,1,0:T(8,128)(2,1)}), bf16[6,256,2048]{2,1,0:T(8,128)(2,1)}) %all-gather.2.cloned.1.call-update) | async-done | bytes 6291472 | tf_op jit(solution)/shard_map/while/body/eval_jaxpr/all_gather | solution.py:70
  1726.7 41.5 %fusion.159 = bf16[1536,2048]{1,0:T(8,128)(2,1)} fusion(bf16[1536,2048]{1,0:T(8,128)(2,1)S(1)} %bitcast.133, bf16[2048,2048]{1,0:T(8,128)(2,1)S(1)} %bitcast.143), kind=kOutput, calls=%fused_computation.15.clone.clone.1.clone.1 | convolution fusion | flops 13089374208 | bytes 20971520 | tf_op jit(solution)/shard_map/while/body/eval_jaxpr/dot_general | solution.py:59
  1807.5 59.7 %reduce-scatter.2.cloned.1.call-done = bf16[6,64,2048]{2,1,0:T(8,128)(2,1)} async-done(((bf16[6,256,2048]{2,1,0:T(8,128)(2,1)}), bf16[6,64,2048]{2,1,0:T(8,128)(2,1)}) %reduce-scatter.2.cloned.1.call-update) | async-done | bytes 1572880 | tf_op jit(solution)/shard_map/while/body/eval_jaxpr/reduce_scatter | solution.py:72
  1881.8 78.0 %all-gather.2.cloned.1.call-done = bf16[6,256,2048]{2,1,0:T(8,128)(2,1)} async-done(((bf16[6,64,2048]{2,1,0:T(8,128)(2,1)}), bf16[6,256,2048]{2,1,0:T(8,128)(2,1)}) %all-gather.2.cloned.1.call-update) | async-done | bytes 6291472 | tf_op jit(solution)/shard_map/while/body/eval_jaxpr/all_gather | solution.py:70
  1994.7 41.5 %fusion.159 = bf16[1536,2048]{1,0:T(8,128)(2,1)} fusion(bf16[1536,2048]{1,0:T(8,128)(2,1)S(1)} %bitcast.133, bf16[2048,2048]{1,0:T(8,128)(2,1)S(1)} %bitcast.143), kind=kOutput, calls=%fused_computation.15.clone.clone.1.clone.1 | convolution fusion | flops 13089374208 | bytes 20971520 | tf_op jit(solution)/shard_map/while/body/eval_jaxpr/dot_general | solution.py:59
  2075.5 59.7 %reduce-scatter.2.cloned.1.call-done = bf16[6,64,2048]{2,1,0:T(8,128)(2,1)} async-done(((bf16[6,256,2048]{2,1,0:T(8,128)(2,1)}), bf16[6,64,2048]{2,1,0:T(8,128)(2,1)}) %reduce-scatter.2.cloned.1.call-update) | async-done | bytes 1572880 | tf_op jit(solution)/shard_map/while/body/eval_jaxpr/reduce_scatter | solution.py:72
  2149.8 78.0 %all-gather.2.cloned.1.call-done = bf16[6,256,2048]{2,1,0:T(8,128)(2,1)} async-done(((bf16[6,64,2048]{2,1,0:T(8,128)(2,1)}), bf16[6,256,2048]{2,1,0:T(8,128)(2,1)}) %all-gather.2.cloned.1.call-update) | async-done | bytes 6291472 | tf_op jit(solution)/shard_map/while/body/eval_jaxpr/all_gather | solution.py:70
  2262.6 41.5 %fusion.159 = bf16[1536,2048]{1,0:T(8,128)(2,1)} fusion(bf16[1536,2048]{1,0:T(8,128)(2,1)S(1)} %bitcast.133, bf16[2048,2048]{1,0:T(8,128)(2,1)S(1)} %bitcast.143), kind=kOutput, calls=%fused_computation.15.clone.clone.1.clone.1 | convolution fusion | flops 13089374208 | bytes 20971520 | tf_op jit(solution)/shard_map/while/body/eval_jaxpr/dot_general | solution.py:59
  2310.0 17.5 fusion.160
  2343.4 59.7 %reduce-scatter.2.cloned.1.call-done = bf16[6,64,2048]{2,1,0:T(8,128)(2,1)} async-done(((bf16[6,256,2048]{2,1,0:T(8,128)(2,1)}), bf16[6,64,2048]{2,1,0:T(8,128)(2,1)}) %reduce-scatter.2.cloned.1.call-update) | async-done | bytes 1572880 | tf_op jit(solution)/shard_map/while/body/eval_jaxpr/reduce_scatter | solution.py:72
  (576 shorter events, 738.3 us)
Async XLA Ops:
  17.4 66.7 %all-gather.2.cloned.1.call-start = ((), (), s32[]{:S(2)}) async-start(), calls=%async_computation.1 | async-start | bytes 7864320 | tf_op jit(solution)/shard_map/while/body/eval_jaxpr/all_gather | solution.py:70
  20.2 239.2 %reduce-scatter.2.cloned.1.call-start = ((), (), s32[]{:S(2)}) async-start(), calls=%async_computation.2 | async-start | bytes 7864320 | tf_op jit(solution)/shard_map/while/body/eval_jaxpr/reduce_scatter | solution.py:72
  263.5 5.8 collective-permute-start
  269.3 82.8 %all-gather.2.cloned.1.call-start = ((), (), s32[]{:S(2)}) async-start(), calls=%async_computation.1 | async-start | bytes 7864320 | tf_op jit(solution)/shard_map/while/body/eval_jaxpr/all_gather | solution.py:70
  272.1 255.3 %reduce-scatter.2.cloned.1.call-start = ((), (), s32[]{:S(2)}) async-start(), calls=%async_computation.2 | async-start | bytes 7864320 | tf_op jit(solution)/shard_map/while/body/eval_jaxpr/reduce_scatter | solution.py:72
  466.0 61.4 %copy-start.1 = (bf16[6,64,2048]{2,1,0:T(8,128)(2,1)S(1)}, bf16[6,64,2048]{2,1,0:T(8,128)(2,1)}, u32[]{:S(2)}) copy-start(bf16[6,64,2048]{2,1,0:T(8,128)(2,1)} %bitcast_select_fusion.3) | copy-start | bytes 4718596 | tf_op jit(solution)/shard_map/while
  531.5 5.8 collective-permute-start
  537.2 82.8 %all-gather.2.cloned.1.call-start = ((), (), s32[]{:S(2)}) async-start(), calls=%async_computation.1 | async-start | bytes 7864320 | tf_op jit(solution)/shard_map/while/body/eval_jaxpr/all_gather | solution.py:70
  540.0 255.3 %reduce-scatter.2.cloned.1.call-start = ((), (), s32[]{:S(2)}) async-start(), calls=%async_computation.2 | async-start | bytes 7864320 | tf_op jit(solution)/shard_map/while/body/eval_jaxpr/reduce_scatter | solution.py:72
  734.0 61.4 %copy-start.1 = (bf16[6,64,2048]{2,1,0:T(8,128)(2,1)S(1)}, bf16[6,64,2048]{2,1,0:T(8,128)(2,1)}, u32[]{:S(2)}) copy-start(bf16[6,64,2048]{2,1,0:T(8,128)(2,1)} %bitcast_select_fusion.3) | copy-start | bytes 4718596 | tf_op jit(solution)/shard_map/while
  799.4 5.8 collective-permute-start
  805.2 82.8 %all-gather.2.cloned.1.call-start = ((), (), s32[]{:S(2)}) async-start(), calls=%async_computation.1 | async-start | bytes 7864320 | tf_op jit(solution)/shard_map/while/body/eval_jaxpr/all_gather | solution.py:70
  808.0 255.3 %reduce-scatter.2.cloned.1.call-start = ((), (), s32[]{:S(2)}) async-start(), calls=%async_computation.2 | async-start | bytes 7864320 | tf_op jit(solution)/shard_map/while/body/eval_jaxpr/reduce_scatter | solution.py:72
  1001.9 61.4 %copy-start.1 = (bf16[6,64,2048]{2,1,0:T(8,128)(2,1)S(1)}, bf16[6,64,2048]{2,1,0:T(8,128)(2,1)}, u32[]{:S(2)}) copy-start(bf16[6,64,2048]{2,1,0:T(8,128)(2,1)} %bitcast_select_fusion.3) | copy-start | bytes 4718596 | tf_op jit(solution)/shard_map/while
  1067.4 5.8 collective-permute-start
  1073.1 82.8 %all-gather.2.cloned.1.call-start = ((), (), s32[]{:S(2)}) async-start(), calls=%async_computation.1 | async-start | bytes 7864320 | tf_op jit(solution)/shard_map/while/body/eval_jaxpr/all_gather | solution.py:70
  1076.0 255.3 %reduce-scatter.2.cloned.1.call-start = ((), (), s32[]{:S(2)}) async-start(), calls=%async_computation.2 | async-start | bytes 7864320 | tf_op jit(solution)/shard_map/while/body/eval_jaxpr/reduce_scatter | solution.py:72
  1269.9 61.4 %copy-start.1 = (bf16[6,64,2048]{2,1,0:T(8,128)(2,1)S(1)}, bf16[6,64,2048]{2,1,0:T(8,128)(2,1)}, u32[]{:S(2)}) copy-start(bf16[6,64,2048]{2,1,0:T(8,128)(2,1)} %bitcast_select_fusion.3) | copy-start | bytes 4718596 | tf_op jit(solution)/shard_map/while
  1335.4 5.8 collective-permute-start
  1341.1 82.8 %all-gather.2.cloned.1.call-start = ((), (), s32[]{:S(2)}) async-start(), calls=%async_computation.1 | async-start | bytes 7864320 | tf_op jit(solution)/shard_map/while/body/eval_jaxpr/all_gather | solution.py:70
  1343.9 255.3 %reduce-scatter.2.cloned.1.call-start = ((), (), s32[]{:S(2)}) async-start(), calls=%async_computation.2 | async-start | bytes 7864320 | tf_op jit(solution)/shard_map/while/body/eval_jaxpr/reduce_scatter | solution.py:72
  1537.8 61.4 %copy-start.1 = (bf16[6,64,2048]{2,1,0:T(8,128)(2,1)S(1)}, bf16[6,64,2048]{2,1,0:T(8,128)(2,1)}, u32[]{:S(2)}) copy-start(bf16[6,64,2048]{2,1,0:T(8,128)(2,1)} %bitcast_select_fusion.3) | copy-start | bytes 4718596 | tf_op jit(solution)/shard_map/while
  1603.3 5.8 collective-permute-start
  1609.1 82.8 %all-gather.2.cloned.1.call-start = ((), (), s32[]{:S(2)}) async-start(), calls=%async_computation.1 | async-start | bytes 7864320 | tf_op jit(solution)/shard_map/while/body/eval_jaxpr/all_gather | solution.py:70
  1611.9 255.3 %reduce-scatter.2.cloned.1.call-start = ((), (), s32[]{:S(2)}) async-start(), calls=%async_computation.2 | async-start | bytes 7864320 | tf_op jit(solution)/shard_map/while/body/eval_jaxpr/reduce_scatter | solution.py:72
  1871.3 5.8 collective-permute-start
  1877.0 82.8 %all-gather.2.cloned.1.call-start = ((), (), s32[]{:S(2)}) async-start(), calls=%async_computation.1 | async-start | bytes 7864320 | tf_op jit(solution)/shard_map/while/body/eval_jaxpr/all_gather | solution.py:70
  1879.8 255.3 %reduce-scatter.2.cloned.1.call-start = ((), (), s32[]{:S(2)}) async-start(), calls=%async_computation.2 | async-start | bytes 7864320 | tf_op jit(solution)/shard_map/while/body/eval_jaxpr/reduce_scatter | solution.py:72
  2139.2 5.8 collective-permute-start
  2145.0 82.8 %all-gather.2.cloned.1.call-start = ((), (), s32[]{:S(2)}) async-start(), calls=%async_computation.1 | async-start | bytes 7864320 | tf_op jit(solution)/shard_map/while/body/eval_jaxpr/all_gather | solution.py:70
  2147.8 255.3 %reduce-scatter.2.cloned.1.call-start = ((), (), s32[]{:S(2)}) async-start(), calls=%async_computation.2 | async-start | bytes 7864320 | tf_op jit(solution)/shard_map/while/body/eval_jaxpr/reduce_scatter | solution.py:72
  2407.2 5.8 collective-permute-start
  (139 other events, 1042.6 us)
Sparse Core Ops, SparseCore 0:
  20.4 63.6 all-gather.1
  198.3 61.1 reduce-scatter.1
  272.2 79.7 all-gather.1
  466.2 61.1 reduce-scatter.1
  540.2 79.8 all-gather.1
  734.2 61.1 reduce-scatter.1
  808.1 79.8 all-gather.1
  1002.1 61.1 reduce-scatter.1
  1076.1 79.8 all-gather.1
  1270.1 61.1 reduce-scatter.1
  1344.0 79.8 all-gather.1
  1538.0 61.1 reduce-scatter.1
  1612.0 79.8 all-gather.1
  1806.0 61.1 reduce-scatter.1
  1880.0 79.8 all-gather.1
  2073.9 61.1 reduce-scatter.1
  2147.9 79.8 all-gather.1
  2341.9 61.1 reduce-scatter.1
where the time goes:
time: 2440 us; the launch traced here: 2420 us
  waiting for transfers between devices  1260 us (52%)
  matrix products  799 us (33%)
  other arithmetic  199 us (8%)
  local copies, waits for them, and re-layouts  130 us (5%)
    all_gather x9, waiting for transfers between devices, stage_layer(): x_full = lax.all_gather(x_shard, 'tp', axis=1, tiled=True)  686 us
    reduce_scatter x9, waiting for transfers between devices, stage_layer(): lax.psum_scatter(partial_sum, 'tp', scatter_dimension=1, tiled=True)  537 us
    dot_general x9, matrix products, branch_partial(): jnp.dot(h_mlp, w_up, preferred_element_type=jnp.float32)  373 us
    dot_general x9, matrix products, branch_partial(): jnp.dot(hidden, w_down, preferred_element_type=jnp.float32)  157 us
    dot_general x9, matrix products, branch_partial(): jnp.einsum('bktgh,kghd->btd', context, w_o, preferred_element_type=jnp.fl...  128 us
    while x288, local copies, waits for them, and re-layouts  63.6 us
    dot_general x9, matrix products, branch_partial(): jnp.dot(h_attn, w_k.reshape(d_model, -1), preferred_element_type=jnp.floa...  57.4 us
    convert_element_type x9, other arithmetic, layer_norm(): (centred * lax.rsqrt(variance + LN_EPS) * ln_gain + ln_bias).astype(jnp.b...  52.7 us
  transfers between devices with their start and end apart: 27, of which 27 were waited for; matrix products, arithmetic and copies ran while one was open for 1% of the time, Pallas kernels for 0%

commit v1 on v0

v1 whole, which is shorter than its diff:
```python
import functools

import jax
import jax.numpy as jnp
import numpy as np
from jax import lax
from jax.experimental import pallas as pl
from jax.experimental.pallas import tpu as pltpu
from jax.sharding import PartitionSpec as P

LN_EPS = 1e-5
ROPE_BASE = 10000.0
MESH = pl.DeviceIdType.MESH
F32 = jnp.float32
BF16 = jnp.bfloat16
COL_TILE = 512
LN_ROWS = 16


def rope_tables(seq_len, head_dim):
    positions = np.arange(seq_len, dtype=np.float32)
    inv_freq = np.float32(ROPE_BASE) ** (np.float32(-2.0) * np.arange(head_dim // 2, dtype=np.float32) / np.float32(head_dim))
    angles = positions[:, None] * inv_freq[None, :]
    cos_tab, sin_tab = np.cos(angles), np.sin(angles)
    return np.concatenate([cos_tab, cos_tab], axis=1), np.concatenate([-sin_tab, sin_tab], axis=1)


def pipeline_kernel(dims, x_in, ln_par, cos_ref, sin_ref, wqkv_hbm, wo_hbm, wup_hbm, wdn_hbm, out_ref,
                    wqkv, wo, wup, wdn, xbuf, yst, pst, rst, rel, fin, ha, hm, hid, qs, kc, vc, ctx,
                    w_sem, own_sem, nb_sem, op_sem, rel_sem, fin_sem, out_sem,
                    x0_send, f_send, wb_send, p_send, r_send, y_send, l_send):
    stages, rows, batch, seq_len, chunk, d_model, heads, hd, ff = dims
    blk = chunk // rows
    halves = seq_len // chunk
    num_chunks = x_in.shape[0] * batch * halves
    half = d_model // 2
    attn = heads * hd
    shard = seq_len // rows
    rows_per_half = rows // halves

    stage = lax.axis_index("pp")
    y = lax.axis_index("tp")
    up_y = lax.rem(y + 1, rows)
    dn_y = lax.rem(y + rows - 1, rows)
    op_y = lax.rem(y + 2, rows)
    first = stage == 0
    last = stage == stages - 1
    nxt = jnp.minimum(stage + 1, stages - 1)
    prv = jnp.maximum(stage - 1, 0)

    def block(row):
        return pl.ds(pl.multiple_of(row * blk, blk), blk)

    col_a, col_b = pl.ds(0, half), pl.ds(half, half)

    def rcopy(src, dst, send, recv, row, stg):
        return pltpu.make_async_remote_copy(src_ref=src, dst_ref=dst, send_sem=send, recv_sem=recv,
                                            device_id={"tp": row, "pp": stg}, device_id_type=MESH)

    weights = [pltpu.make_async_copy(src, dst, w_sem.at[i])
               for i, (src, dst) in enumerate(((wqkv_hbm, wqkv), (wup_hbm, wup), (wo_hbm, wo), (wdn_hbm, wdn)))]
    for copy in weights:
        copy.start()

    barrier = pltpu.get_barrier_semaphore()
    for shift in range(1, rows):
        pl.semaphore_signal(barrier, inc=1, device_id={"tp": lax.rem(y + shift, rows)}, device_id_type=MESH)

    @pl.when(jnp.logical_not(first))
    def _():
        for row in range(rows):
            pl.semaphore_signal(barrier, inc=1, device_id={"tp": row, "pp": prv}, device_id_type=MESH)

    @pl.when(jnp.logical_not(last))
    def _():
        for row in range(rows):
            pl.semaphore_signal(barrier, inc=1, device_id={"tp": row, "pp": nxt}, device_id_type=MESH)

    @pl.when(jnp.logical_or(first, last))
    def _():
        pl.semaphore_wait(barrier, 2 * rows - 1)

    @pl.when(jnp.logical_not(jnp.logical_or(first, last)))
    def _():
        pl.semaphore_wait(barrier, 3 * rows - 1)

    def seq_of(c):
        sigma = c // halves
        return sigma // batch, lax.rem(sigma, batch)

    my_part = lax.rem(y, rows_per_half)
    my_half = y // rows_per_half
    my_rows = pl.ds(pl.multiple_of(my_part * shard, shard), shard)

    def x0_copies(c):
        m, b = seq_of(c)
        slot = lax.rem(c // halves, 2)
        return [rcopy(x_in.at[m, b], xbuf.at[c, my_rows], x0_send.at[slot, i], own_sem.at[c],
                      lax.rem(y + 1 + i, rows), stage) for i in range(rows - 1)]

    def x0_issue(c):
        @pl.when(jnp.logical_and(first, my_half == lax.rem(c, halves)))
        def _():
            @pl.when(c >= 2 * halves)
            def _():
                for copy in x0_copies(c - 2 * halves):
                    copy.wait_send()
            for copy in x0_copies(c):
                copy.start()
            m, b = seq_of(c)
            pltpu.make_async_copy(x_in.at[m, b], xbuf.at[c, my_rows], own_sem.at[c]).start()

    def forwards(c):
        slot = lax.rem(c, 2)
        return [rcopy(xbuf.at[c, block(dn_y), col_a], xbuf.at[c, block(dn_y), col_a], f_send.at[slot, 0], op_sem.at[c], up_y, stage),
                rcopy(xbuf.at[c, block(up_y), col_b], xbuf.at[c, block(up_y), col_b], f_send.at[slot, 1], op_sem.at[c], dn_y, stage)]

    def wait_block(c, row, sem):
        ref = xbuf.at[c, block(row)]
        rcopy(ref, ref, f_send.at[0, 0], sem, up_y, stage).wait_recv()

    def relay_x(c):
        @pl.when(jnp.logical_not(first))
        def _():
            @pl.when(c >= 2)
            def _():
                for copy in forwards(c - 2):
                    copy.wait_send()
            fwd = forwards(c)
            wait_block(c, dn_y, nb_sem.at[c, 0])
            fwd[0].start()
            wait_block(c, up_y, nb_sem.at[c, 1])
            fwd[1].start()

    def wb_copy(c):
        m, b = seq_of(c)
        return rcopy(xbuf.at[c, my_rows], out_ref.at[0, m, b], wb_send.at[lax.rem(c // halves, 2)], out_sem.at[0], y, prv)

    def wait_x(c):
        @pl.when(first)
        def _():
            ref = xbuf.at[c]
            rcopy(ref, ref, f_send.at[0, 0], own_sem.at[c], up_y, stage).wait_recv()

        @pl.when(jnp.logical_not(first))
        def _():
            wait_block(c, y, own_sem.at[c])
            wait_block(c, op_y, op_sem.at[c])

            @pl.when(my_half == lax.rem(c, halves))
            def _():
                @pl.when(c >= 2 * halves)
                def _():
                    wb_copy(c - 2 * halves).wait_send()
                wb_copy(c).start()

    def p_copies(c):
        p = lax.rem(c, 2)
        return [rcopy(pst.at[p, block(op_y), col_a], rel.at[c, 0], p_send.at[p, 0], rel_sem.at[c, 0], dn_y, stage),
                rcopy(pst.at[p, block(up_y), col_a], fin.at[c, 1, :, col_a], p_send.at[p, 1], fin_sem.at[c], up_y, stage),
                rcopy(pst.at[p, block(op_y), col_b], rel.at[c, 1], p_send.at[p, 2], rel_sem.at[c, 1], up_y, stage),
                rcopy(pst.at[p, block(dn_y), col_b], fin.at[c, 0, :, col_b], p_send.at[p, 3], fin_sem.at[c], dn_y, stage)]

    def r_copies(c):
        p = lax.rem(c, 2)
        return [rcopy(rst.at[p, 0], fin.at[c, 0, :, col_a], r_send.at[p, 0], fin_sem.at[c], dn_y, stage),
                rcopy(rst.at[p, 1], fin.at[c, 1, :, col_b], r_send.at[p, 1], fin_sem.at[c], up_y, stage)]

    def relay_sums(c):
        p = lax.rem(c, 2)

        @pl.when(c >= 2)
        def _():
            for copy in r_copies(c - 2):
                copy.wait_send()
        out = r_copies(c)
        for i, (row, col) in enumerate(((dn_y, col_a), (up_y, col_b))):
            ref = rel.at[c, i]
            rcopy(ref, ref, r_send.at[0, i], rel_sem.at[c, i], up_y, stage).wait_recv()
            rst[p, i] = (rel[c, i].astype(F32) + pst[p, block(row), col].astype(F32)).astype(BF16)
            out[i].start()

    def y_copies(c):
        slot = lax.rem(c, 2)
        return [rcopy(yst.at[c], xbuf.at[c, block(y)], y_send.at[slot, 0], nb_sem.at[c, 0], up_y, nxt),
                rcopy(yst.at[c], xbuf.at[c, block(y)], y_send.at[slot, 1], nb_sem.at[c, 1], dn_y, nxt),
                rcopy(yst.at[c], xbuf.at[c, block(y)], y_send.at[slot, 2], own_sem.at[c], y, nxt)]

    def last_place(c):
        m, b = seq_of(c)
        token = lax.rem(c, halves) * chunk + y * blk
        row = token // shard
        start = pl.multiple_of(lax.rem(token, shard), blk)
        return row, out_ref.at[0, m, b, pl.ds(start, blk)]

    def last_copy(c):
        row, dst = last_place(c)
        return rcopy(yst.at[c], dst, l_send.at[lax.rem(c, 2)], out_sem.at[0], row, stage)

    def last_is_remote(c):
        return last_place(c)[0] != y

    def finish(c):
        p = lax.rem(c, 2)
        ref = fin.at[c]
        rcopy(ref, ref, r_send.at[0, 0], fin_sem.at[c], up_y, stage).wait_recv()
        total = xbuf[c, block(y)].astype(F32) + pst[p, block(y)].astype(F32)
        yst[c] = (total + fin[c, 0].astype(F32) + fin[c, 1].astype(F32)).astype(BF16)

        @pl.when(jnp.logical_not(last))
        def _():
            @pl.when(c >= 2)
            def _():
                for copy in y_copies(c - 2):
                    copy.wait_send()
            for copy in y_copies(c):
                copy.start()

        @pl.when(last)
        def _():
            @pl.when(jnp.logical_and(c >= 2, last_is_remote(c - 2)))
            def _():
                last_copy(c - 2).wait_send()

            @pl.when(last_is_remote(c))
            def _():
                last_copy(c).start()

            @pl.when(jnp.logical_not(last_is_remote(c)))
            def _():
                pltpu.make_async_copy(yst.at[c], last_place(c)[1], out_sem.at[0]).start()

    def norms(c):
        gain_a, bias_a = ln_par[0:1, :], ln_par[1:2, :]
        gain_m, bias_m = ln_par[2:3, :], ln_par[3:4, :]
        for start in range(0, chunk, LN_ROWS):
            part = pl.ds(start, LN_ROWS)
            x = xbuf[c, part].astype(F32)
            centred = x - jnp.mean(x, axis=-1, keepdims=True)
            scale = lax.rsqrt(jnp.mean(centred * centred, axis=-1, keepdims=True) + LN_EPS)
            normed = centred * scale
            ha[part] = (normed * gain_a + bias_a).astype(BF16)
            hm[part] = (normed * gain_m + bias_m).astype(BF16)

    def project(c):
        start = pl.multiple_of(lax.rem(c, halves) * chunk, chunk)
        where = pl.ds(start, chunk)
        cos, sin = cos_ref[where], sin_ref[where]

        def rope(val):
            turned = jnp.concatenate([val[:, hd // 2:], val[:, :hd // 2]], axis=1)
            return (val * cos + turned * sin).astype(BF16)

        h = ha[...]
        q = jnp.dot(h, wqkv[:, 0:attn], preferred_element_type=F32)
        for i in range(heads):
            qs[:, i * hd:(i + 1) * hd] = rope(q[:, i * hd:(i + 1) * hd])
        k = jnp.dot(h, wqkv[:, attn:2 * attn], preferred_element_type=F32)
        for i in range(heads):
            kc[where, i * hd:(i + 1) * hd] = rope(k[:, i * hd:(i + 1) * hd])
        vc[where, :] = jnp.dot(h, wqkv[:, 2 * attn:3 * attn], preferred_element_type=F32).astype(BF16)

    def attention(c):
        row_pos = lax.rem(c, halves) * chunk + lax.broadcasted_iota(jnp.int32, (chunk, seq_len), 0)
        allowed = row_pos >= lax.broadcasted_iota(jnp.int32, (chunk, seq_len), 1)
        for i in range(heads):
            cols = slice(i * hd, (i + 1) * hd)
            scores = lax.dot_general(qs[:, cols], kc[:, cols], (((1,), (1,)), ((), ())), preferred_element_type=F32) * (hd ** -0.5)
            scores = jnp.where(allowed, scores, -1e30)
            weights_ = jnp.exp(scores - jnp.max(scores, axis=-1, keepdims=True))
            probs = (weights_ / jnp.sum(weights_, axis=-1, keepdims=True)).astype(BF16)
            ctx[:, cols] = jnp.dot(probs, vc[:, cols], preferred_element_type=F32).astype(BF16)

    def mlp_up():
        h = hm[...]
        for start in range(0, ff, COL_TILE):
            cols = slice(start, start + COL_TILE)
            u = jnp.dot(h, wup[:, cols], preferred_element_type=F32)
            hid[:, cols] = (0.5 * u * (1.0 + lax.erf(u * np.float32(0.5 ** 0.5)))).astype(BF16)

    def down(c, begin, end):
        p = lax.rem(c, 2)
        a, h = ctx[...], hid[...]
        for start in range(begin, end, COL_TILE):
            cols = slice(start, start + COL_TILE)
            out = jnp.dot(a, wo[:, cols], preferred_element_type=F32) + jnp.dot(h, wdn[:, cols], preferred_element_type=F32)
            pst[p, :, cols] = out.astype(BF16)

    kc[...] = jnp.zeros_like(kc)
    vc[...] = jnp.zeros_like(vc)
    lead = min(3, num_chunks)
    for c in range(lead):
        x0_issue(jnp.int32(c))
    for copy in weights:
        copy.wait()

    def step(c, carry):
        relay_x(c)

        @pl.when(c + lead < num_chunks)
        def _():
            x0_issue(c + lead)
        wait_x(c)
        norms(c)
        project(c)

        @pl.when(c >= 1)
        def _():
            finish(c - 1)
        attention(c)
        mlp_up()

        @pl.when(c >= 2)
        def _():
            for copy in p_copies(c - 2):
                copy.wait_send()
        down(c, 0, half)
        sends = p_copies(c)
        sends[0].start()
        sends[1].start()
        down(c, half, d_model)
        sends[2].start()
        sends[3].start()
        relay_sums(c)
        return carry

    lax.fori_loop(0, num_chunks, step, 0)
    finish(jnp.int32(num_chunks - 1))

    for c in (num_chunks - 2, num_chunks - 1):
        c = jnp.int32(c)
        for copy in p_copies(c) + r_copies(c):
            copy.wait_send()

        @pl.when(jnp.logical_not(first))
        def _():
            for copy in forwards(c):
                copy.wait_send()

        @pl.when(jnp.logical_not(last))
        def _():
            for copy in y_copies(c):
                copy.wait_send()

        @pl.when(jnp.logical_and(last, last_is_remote(c)))
        def _():
            last_copy(c).wait_send()
    for back in (2, 1):
        c = num_chunks - back * halves + my_half

        @pl.when(first)
        def _():
            for copy in x0_copies(c):
                copy.wait_send()

        @pl.when(jnp.logical_not(first))
        def _():
            wb_copy(c).wait_send()
    whole = out_ref.at[0]
    rcopy(whole, whole, l_send.at[0], out_sem.at[0], up_y, stage).wait_recv()


def solution(mesh):
    stages, rows = mesh.shape["pp"], mesh.shape["tp"]

    def stage_body(x_in, ln_params, w_q, w_k, w_v, w_o, w_up, w_down):
        num_micro, batch, shard, d_model = x_in.shape
        heads, hd = w_k.shape[2:]
        ff = w_up.shape[2]
        attn = heads * hd
        seq_len = shard * rows
        chunk = seq_len // 2
        blk = chunk // rows
        halves = seq_len // chunk
        num_chunks = num_micro * batch * halves
        half = d_model // 2
        w_qkv = jnp.concatenate([w.reshape(d_model, attn) for w in (w_q, w_k, w_v)], axis=1)
        cos_tab, sin_tab = rope_tables(seq_len, hd)
        dims = (stages, rows, batch, seq_len, chunk, d_model, heads, hd, ff)
        hbm = pl.BlockSpec(memory_space=pl.ANY)
        vmem = pl.BlockSpec(memory_space=pltpu.VMEM)
        dma = pltpu.SemaphoreType.DMA
        return pl.pallas_call(
            functools.partial(pipeline_kernel, dims),
            out_shape=jax.ShapeDtypeStruct((1,) + x_in.shape, BF16),
            in_specs=[hbm, vmem, vmem, vmem, hbm, hbm, hbm, hbm],
            out_specs=hbm,
            scratch_shapes=[
                pltpu.VMEM((d_model, 3 * attn), BF16),
                pltpu.VMEM((attn, d_model), BF16),
                pltpu.VMEM((d_model, ff), BF16),
                pltpu.VMEM((ff, d_model), BF16),
                pltpu.VMEM((num_chunks, chunk, d_model), BF16),
                pltpu.VMEM((num_chunks, blk, d_model), BF16),
                pltpu.VMEM((2, chunk, d_model), BF16),
                pltpu.VMEM((2, 2, blk, half), BF16),
                pltpu.VMEM((num_chunks, 2, blk, half), BF16),
                pltpu.VMEM((num_chunks, 2, blk, d_model), BF16),
                pltpu.VMEM((chunk, d_model), BF16),
                pltpu.VMEM((chunk, d_model), BF16),
                pltpu.VMEM((chunk, ff), BF16),
                pltpu.VMEM((chunk, attn), BF16),
                pltpu.VMEM((seq_len, attn), BF16),
                pltpu.VMEM((seq_len, attn), BF16),
                pltpu.VMEM((chunk, attn), BF16),
                dma((4,)),
                dma((num_chunks,)),
                dma((num_chunks, 2)),
                dma((num_chunks,)),
                dma((num_chunks, 2)),
                dma((num_chunks,)),
                dma((1,)),
                dma((2, rows - 1)),
                dma((2, 2)),
                dma((2,)),
                dma((2, 4)),
                dma((2, 2)),
                dma((2, 3)),
                dma((2,)),
            ],
            compiler_params=pltpu.CompilerParams(collective_id=0, has_side_effects=True, vmem_limit_bytes=67_000_000),
        )(x_in, ln_params[0], cos_tab, sin_tab, w_qkv, w_o.reshape(attn, d_model), w_up[0], w_down[0])

    in_specs = (P(None, "dp", "tp", None), P("pp", None, None), P("pp", None, "tp", None, None), P("pp", None, "tp", None), P("pp", None, "tp", None), P("pp", "tp", None, None, None), P("pp", None, "tp"), P("pp", "tp", None))
    return jax.shard_map(stage_body, mesh=mesh, in_specs=in_specs, out_specs=P("pp", None, "dp", "tp", None), check_vma=False)
```

time: 2440 us -> 538 us (0.22)
  waiting for transfers between devices: 1260 us -> 0 us
  matrix products: 799 us -> 0 us
  Pallas kernels: 0 us -> 527 us
  other arithmetic: 199 us -> 2.99 us
  local copies, waits for them, and re-layouts: 130 us -> 7.65 us
    dot_general x63 -> x0, matrix products: 799 us -> none  [the longest x9 373 us: branch_partial(): jnp.dot(h_mlp, w_up, preferred_element_type=jnp.float32)]
    all_gather x9 -> x0, waiting for transfers between devices: 686 us -> none  [stage_layer(): x_full = lax.all_gather(x_shard, 'tp', axis=1, tiled=True)]
    reduce_scatter x9 -> x0, waiting for transfers between devices: 537 us -> none  [stage_layer(): lax.psum_scatter(partial_sum, 'tp', scatter_dimension=1, tiled=True)]
    pallas_call x0 -> x1, Pallas kernels: none -> 527 us  [stage_body(): pl.pallas_call(functools.partial(pipeline_kernel, dims), out_shape=jax.Sh...]
    while x290 -> x0, local copies, waits for them, and re-layouts: 72.2 us -> none
    convert_element_type x9 -> x0, other arithmetic: 52.7 us -> none  [layer_norm(): (centred * lax.rsqrt(variance + LN_EPS) * ln_gain + ln_bias).astype(jnp.b...]
    reduce_sum x18 -> x0, other arithmetic: 50.4 us -> none  [the longest x9 34.4 us: layer_norm(): row_mean = jnp.mean(x_f32, axis=-1, keepdims=True)]
    ppermute x9 -> x0, waiting for transfers between devices: 40 us -> none  [micro_step(): recv_buf = lax.ppermute(layer_out, 'pp', send_pairs)]
  transfers between devices with their start and end apart: 27 -> 0, of which waited for: 27 -> 0; matrix products, arithmetic and copies ran while one was open for 1% -> 0% of each run, Pallas kernels for 0% -> 0%
where the time goes in v1:
time: 538 us
  Pallas kernels  527 us (98%)
  local copies, waits for them, and re-layouts  7.65 us (1%)
    pallas_call x1, Pallas kernels, stage_body(): pl.pallas_call(functools.partial(pipeline_kernel, dims), out_shape=jax.Sh...  527 us

profile of v1, /device:TPU:119, one launch (start us, length us, event | category | flops | bytes accessed | tf_op | source)
XLA Modules:
  0.0 537.7 jit_solution(13913584820916256829)
XLA Ops:
  0.0 0.0 copy-start
  0.0 0.0 copy-start.1
  0.0 2.1 copy.17
  2.1 0.1 copy-done
  2.2 0.6 copy-done.1
  2.9 0.8 copy_bitcast_fusion
  3.7 3.0 pad_maximum_fusion.wqkv_hbm
  6.7 527.1 %shard_map.100 = bf16[1,2,6,64,2048]{4,3,2,1,0:T(8,128)(2,1)} custom-call(bf16[2,6,64,2048]{3,2,1,0:T(8,128)(2,1)} %x_in.1, f32[4,2048]{1,0:T(4,128)} %bitcast.25, f32[256,128]{1,0:T(8,128)} %constant.4.clone.cos_ref, f32[256,128]{1,0:T(8,128)} %constant.5.clone.sin_ref, bf16[2048,1536]{1,0:T(8,128)(2,1)} %pad_maximum_fusion.wqkv_hbm, ...), custom_call_target="tpu_custom_call" | custom-call | tf_op jit(solution)/shard_map/pallas_call | solution.py:383
  533.7 4.0 copy.19
Async XLA Ops:
  0.0 2.2 copy-start
  0.0 2.9 copy-start.1

commit v2 on v0

v2 whole, which is shorter than its diff:
```python
import functools

import jax
import jax.numpy as jnp
import numpy as np
from jax import lax
from jax.experimental import pallas as pl
from jax.experimental.pallas import tpu as pltpu
from jax.sharding import PartitionSpec as P

LN_EPS = 1e-5
ROPE_BASE = 10000.0
MESH = pl.DeviceIdType.MESH
F32 = jnp.float32
BF16 = jnp.bfloat16
COL_TILE = 512
TILES = 2
HALVES = 2
SLOTS = 2
DIRECT = 8
ORDER = ("W", "N", "Q", "s-1", "t-1", "Z", "x-2o", "y-2o", "a", "b", "F-1", "G-1")
LN_ROWS = 16


def rope_tables(seq_len, head_dim):
    positions = np.arange(seq_len, dtype=np.float32)
    inv_freq = np.float32(ROPE_BASE) ** (np.float32(-2.0) * np.arange(head_dim // 2, dtype=np.float32) / np.float32(head_dim))
    angles = positions[:, None] * inv_freq[None, :]
    cos_tab, sin_tab = np.cos(angles), np.sin(angles)
    return np.concatenate([cos_tab, cos_tab], axis=1), np.concatenate([-sin_tab, sin_tab], axis=1)


def pipeline_kernel(dims, x_in, ln_par, cos_ref, sin_ref, wq_hbm, wk_hbm, wv_hbm, wo_hbm, wup_hbm, wdn_hbm, out_ref, gbuf,
                    wqkv, wup, wod, xbuf, yst, pst, sst, rec1, rec2, ha, hm, act, qs, kc, vc,
                    w_sem, x_sem, one_sem, two_sem, cr_sem, out_sem, x0_send, g_sem, g_send, wb_send, p_send, s_send, y_send, l_send, c_send):
    stages, rows, batch, seq_len, chunk, d_model, heads, hd, ff = dims
    halves = seq_len // chunk
    num_chunks = x_in.shape[0] * batch * halves
    seqs = num_chunks // halves
    half = d_model // 2
    tile = half // TILES
    attn = heads * hd
    shard = seq_len // rows
    per = rows // halves
    sb = chunk // 2

    stage = lax.axis_index("pp")
    y = lax.axis_index("tp")
    first = stage == 0
    last = stage == stages - 1
    nxt = jnp.minimum(stage + 1, stages - 1)
    prv = jnp.maximum(stage - 1, 0)
    others = [lax.rem(y + shift, rows) for shift in range(1, rows)]
    odd = lax.rem(stage, 2) == 1
    turning = jnp.logical_and(odd, jnp.logical_not(last))

    flip, mirror = y + 1 - 2 * lax.rem(y, 2), rows - 1 - y
    partner, cross = (flip, mirror), (mirror, flip)

    def share(row, k):
        return row // 2 if k == 0 else jnp.where(jnp.logical_or(row == 1, row == 2), 1, 0)

    def tokens(index):
        return pl.ds(pl.multiple_of(index * sb, sb), sb)

    def rows_of(row):
        return pl.ds(pl.multiple_of(row * shard, shard), shard)

    def within(row):
        return rows_of(lax.rem(row, per))

    col = (pl.ds(0, half), pl.ds(half, half))

    def rcopy(src, dst, send, recv, row, stg):
        return pltpu.make_async_remote_copy(src_ref=src, dst_ref=dst, send_sem=send, recv_sem=recv,
                                            device_id={"tp": row, "pp": stg}, device_id_type=MESH)

    def arrived(ref, sem):
        rcopy(ref, ref, sem, sem, others[0], stage).wait_recv()

    places = [(src, wqkv.at[:, pl.ds(i * attn, attn)]) for i, src in enumerate((wq_hbm, wk_hbm, wv_hbm))]
    places += [(wup_hbm, wup), (wo_hbm, wod.at[pl.ds(0, attn)]), (wdn_hbm, wod.at[pl.ds(attn, ff)])]
    weights = [pltpu.make_async_copy(src, dst, w_sem.at[i]) for i, (src, dst) in enumerate(places)]
    for copy in weights:
        copy.start()

    barrier = pltpu.get_barrier_semaphore()
    for row in others:
        pl.semaphore_signal(barrier, inc=1, device_id={"tp": row}, device_id_type=MESH)

    @pl.when(jnp.logical_not(first))
    def _():
        for row in range(rows):
            pl.semaphore_signal(barrier, inc=1, device_id={"tp": row, "pp": prv}, device_id_type=MESH)

    @pl.when(jnp.logical_not(last))
    def _():
        for row in range(rows):
            pl.semaphore_signal(barrier, inc=1, device_id={"tp": row, "pp": nxt}, device_id_type=MESH)

    @pl.when(jnp.logical_or(first, last))
    def _():
        pl.semaphore_signal(barrier, inc=1, device_id={"tp": y, "pp": jnp.where(first, stages - 1, 0)}, device_id_type=MESH)
        pl.semaphore_wait(barrier, 2 * rows)

    @pl.when(jnp.logical_not(jnp.logical_or(first, last)))
    def _():
        pl.semaphore_wait(barrier, 3 * rows - 1)

    def seq_of(c):
        sigma = c // halves
        return sigma // batch, lax.rem(sigma, batch)

    my_rows = within(y)

    def owns(c):
        return y // per == lax.rem(c, halves)

    def x0_local(c):
        m, b = seq_of(c)
        return pltpu.make_async_copy(x_in.at[m, b], xbuf.at[c, my_rows], x_sem.at[c])

    def x0_copies(c):
        m, b = seq_of(c)
        return [rcopy(x_in.at[m, b], xbuf.at[c, my_rows], x0_send.at[i], x_sem.at[c], row, stage) for i, row in enumerate(others)]

    def g_exchange(sigma):
        m, b = sigma // batch, sigma % batch
        return [rcopy(x_in.at[m, b], gbuf.at[sigma, rows_of(y)], g_send.at[0], g_sem.at[sigma], row, stage) for row in others]

    def g_pass(sigma):
        out = []
        for row in others:
            c = sigma * halves + row // per
            out.append(rcopy(gbuf.at[sigma, rows_of(row)], xbuf.at[c, within(row)], g_send.at[1], x_sem.at[c], y, 0))
        return out

    def feed():
        @pl.when(first)
        def _():
            for c in range(halves):
                @pl.when(owns(c))
                def _():
                    for copy in x0_copies(jnp.int32(c)):
                        copy.start()
            for c in range(num_chunks):
                @pl.when(owns(c))
                def _():
                    x0_local(jnp.int32(c)).start()

        @pl.when(last)
        def _():
            for sigma in range(1, seqs):
                for copy in g_exchange(sigma):
                    copy.start()
            for sigma in range(1, seqs):
                arrived(gbuf.at[sigma, pl.ds(0, seq_len - shard)], g_sem.at[sigma])
                for copy in g_pass(sigma):
                    copy.start()

    def wb_copy(c):
        m, b = seq_of(c)
        return rcopy(xbuf.at[c, my_rows], out_ref.at[0, m, b], wb_send.at[lax.rem(c // halves, 2)], out_sem.at[0], y, prv)

    def wait_x(c):
        arrived(xbuf.at[c], x_sem.at[c])

        @pl.when(jnp.logical_and(jnp.logical_not(first), owns(c)))
        def _():
            @pl.when(jnp.logical_and(c >= 2 * halves, jnp.logical_not(odd)))
            def _():
                wb_copy(c - 2 * halves).wait_send()
            wb_copy(c).start()

    def p_copies(c, k):
        p = lax.rem(c, SLOTS)
        out = []
        for i in range(TILES):
            cols = pl.ds(k * half + i * tile, tile)
            out.append(rcopy(pst.at[p, tokens(share(cross[k], k)), cols], rec1.at[c, k, :, pl.ds(i * tile, tile)],
                             p_send.at[p, k * TILES + i], one_sem.at[c, k], cross[k], stage))
        return out

    def s_copy(c, k):
        p = lax.rem(c, SLOTS)
        return rcopy(sst.at[p, k], rec2.at[c, k], s_send.at[p, k], two_sem.at[c, k], partner[k], stage)

    def first_sum(c, k):
        p = lax.rem(c, SLOTS)

        @pl.when(c >= SLOTS)
        def _():
            s_copy(c - SLOTS, k).wait_send()
        arrived(rec1.at[c, k], one_sem.at[c, k])
        own = pst[p, tokens(share(y, k)), col[k]]
        sst[p, k] = (rec1[c, k].astype(F32) + own.astype(F32)).astype(BF16)
        s_copy(c, k).start()

    def y_copies(c, k, around):
        p = lax.rem(c, SLOTS)
        where = (c, tokens(share(y, k)), col[k])
        side = rcopy(yst.at[p, k], xbuf.at[where], y_send.at[p, k, 0], cr_sem.at[c, k] if around else x_sem.at[c], cross[k], stage if around else nxt)
        return [side, rcopy(yst.at[p, k], xbuf.at[where], y_send.at[p, k, 1], x_sem.at[c], y, nxt)]

    def c_copy(c, k):
        ref = xbuf.at[c, tokens(share(cross[k], k)), col[k]]
        return rcopy(ref, ref, c_send.at[lax.rem(c, SLOTS), k], x_sem.at[c], y, nxt)

    def carry(c, k):
        @pl.when(jnp.logical_and(turning, c >= DIRECT))
        def _():
            @pl.when(c >= DIRECT + SLOTS)
            def _():
                c_copy(c - SLOTS, k).wait_send()
            arrived(xbuf.at[c, tokens(share(cross[k], k)), col[k]], cr_sem.at[c, k])
            c_copy(c, k).start()

    def last_place(c, k):
        token = lax.rem(c, halves) * chunk + share(y, k) * sb
        start = pl.multiple_of(lax.rem(token, shard), sb)
        m, b = seq_of(c)
        return token // shard, out_ref.at[0, m, b, pl.ds(start, sb), col[k]]

    def last_do(c, k, remote, local):
        p = lax.rem(c, SLOTS)
        row, dst = last_place(c, k)

        @pl.when(row == cross[k])
        def _():
            remote(rcopy(yst.at[p, k], dst, l_send.at[p, k], out_sem.at[k], cross[k], stage))

        @pl.when(row == y)
        def _():
            local(pltpu.make_async_copy(yst.at[p, k], dst, l_send.at[p, k]))

    def finish_half(c, k):
        p = lax.rem(c, SLOTS)

        @pl.when(jnp.logical_and(c >= SLOTS, jnp.logical_not(last)))
        def _():
            for copy in y_copies(c - SLOTS, k, False):
                copy.wait_send()

        @pl.when(jnp.logical_and(c >= SLOTS, last))
        def _():
            last_do(c - SLOTS, k, lambda copy: copy.wait_send(), lambda copy: copy.wait())
        arrived(rec2.at[c, k], two_sem.at[c, k])
        total = sst[p, k].astype(F32) + rec2[c, k].astype(F32)
        yst[p, k] = (xbuf[c, tokens(share(y, k)), col[k]].astype(F32) + total).astype(BF16)

        around = jnp.logical_and(turning, c >= DIRECT)

        @pl.when(around)
        def _():
            for copy in y_copies(c, k, True):
                copy.start()

        @pl.when(jnp.logical_not(jnp.logical_or(around, last)))
        def _():
            for copy in y_copies(c, k, False):
                copy.start()

        @pl.when(last)
        def _():
            last_do(c, k, lambda copy: copy.start(), lambda copy: copy.start())

    def norms(c):
        gain_a, bias_a = ln_par[0:1, :], ln_par[1:2, :]
        gain_m, bias_m = ln_par[2:3, :], ln_par[3:4, :]
        for start in range(0, chunk, LN_ROWS):
            part = pl.ds(start, LN_ROWS)
            x = xbuf[c, part].astype(F32)
            centred = x - jnp.mean(x, axis=-1, keepdims=True)
            scale = lax.rsqrt(jnp.mean(centred * centred, axis=-1, keepdims=True) + LN_EPS)
            normed = centred * scale
            ha[part] = (normed * gain_a + bias_a).astype(BF16)
            hm[part] = (normed * gain_m + bias_m).astype(BF16)

    def project(c):
        start = pl.multiple_of(lax.rem(c, halves) * chunk, chunk)
        where = pl.ds(start, chunk)
        cos, sin = cos_ref[where], sin_ref[where]

        def rope(val):
            turned = jnp.concatenate([val[:, hd // 2:], val[:, :hd // 2]], axis=1)
            return (val * cos + turned * sin).astype(BF16)

        h = ha[...]
        q = jnp.dot(h, wqkv[:, 0:attn], preferred_element_type=F32)
        for i in range(heads):
            qs[:, i * hd:(i + 1) * hd] = rope(q[:, i * hd:(i + 1) * hd])
        k = jnp.dot(h, wqkv[:, attn:2 * attn], preferred_element_type=F32)
        for i in range(heads):
            kc[where, i * hd:(i + 1) * hd] = rope(k[:, i * hd:(i + 1) * hd])
        vc[where, :] = jnp.dot(h, wqkv[:, 2 * attn:3 * attn], preferred_element_type=F32).astype(BF16)

    def attend(c, i):
        row_pos = lax.rem(c, halves) * chunk + lax.broadcasted_iota(jnp.int32, (chunk, seq_len), 0)
        allowed = row_pos >= lax.broadcasted_iota(jnp.int32, (chunk, seq_len), 1)
        cols = slice(i * hd, (i + 1) * hd)
        scores = lax.dot_general(qs[:, cols], kc[:, cols], (((1,), (1,)), ((), ())), preferred_element_type=F32) * (hd ** -0.5)
        scores = jnp.where(allowed, scores, -1e30)
        weights_ = jnp.exp(scores - jnp.max(scores, axis=-1, keepdims=True))
        return (weights_ / jnp.sum(weights_, axis=-1, keepdims=True)).astype(BF16)

    def contract(i, probs):
        cols = slice(i * hd, (i + 1) * hd)
        act[:, cols] = jnp.dot(probs, vc[:, cols], preferred_element_type=F32).astype(BF16)

    def attention(c):
        for i in range(heads):
            contract(i, attend(c, i))

    def up_tile(i, width):
        cols = slice(i * width, (i + 1) * width)
        u = jnp.dot(hm[...], wup[:, cols], preferred_element_type=F32)
        act[:, attn + i * width:attn + (i + 1) * width] = (0.5 * u * (1.0 + lax.erf(u * np.float32(0.5 ** 0.5)))).astype(BF16)

    def mlp_up():
        for i in range(ff // COL_TILE):
            up_tile(i, COL_TILE)

    def attention_and_up(c):
        for i in range(heads):
            probs = attend(c, i)
            up_tile(i, ff // heads)
            contract(i, probs)

    def down(c, k):
        p = lax.rem(c, SLOTS)
        a = act[...]
        copies = p_copies(c, k)
        for i, start in enumerate(range(k * half, (k + 1) * half, tile)):
            cols = slice(start, start + tile)
            out = jnp.dot(a, wod[:, cols], preferred_element_type=F32)
            pst[p, :, cols] = out.astype(BF16)
            copies[i].start()

    kc[...] = jnp.zeros_like(kc)
    vc[...] = jnp.zeros_like(vc)
    feed()

    def loaded(c, which):
        @pl.when(c == 0)
        def _():
            for copy in which:
                copy.wait()

    def project_first(c):
        loaded(c, weights[:3])
        project(c)

    def mlp_up_first(c):
        loaded(c, weights[3:4])
        mlp_up()

    def both(c):
        loaded(c, weights[3:4])
        attention_and_up(c)

    def down_a(c):
        loaded(c, weights[4:])

        @pl.when(c >= SLOTS)
        def _():
            for k in range(2):
                for copy in p_copies(c - SLOTS, k):
                    copy.wait_send()

        @pl.when(jnp.logical_and(odd, owns(c)))
        def _():
            wb_copy(c).wait_send()
        down(c, 0)

    acts = {"W": wait_x, "N": norms, "Q": project_first, "A": attention, "U": mlp_up_first, "Z": both, "a": down_a, "b": lambda c: down(c, 1),
            "s": lambda c: first_sum(c, 0), "t": lambda c: first_sum(c, 1), "x": lambda c: carry(c, 0), "y": lambda c: carry(c, 1), "F": lambda c: finish_half(c, 0), "G": lambda c: finish_half(c, 1)}
    order = [(o[0], int(o[1:].rstrip("eo") or 0), {"e": jnp.logical_not(odd), "o": odd}.get(o[-1])) for o in ORDER]

    def guarded(ok, fn, c):
        @pl.when(ok)
        def _():
            fn(c)

    def step(c, carry):
        for name, shift, which in order:
            fn = acts[name]
            if shift < 0:
                ok = c + shift >= 0
                guarded(ok if which is None else jnp.logical_and(ok, which), fn, c + shift)
            elif which is not None:
                guarded(which, fn, c)
            else:
                fn(c)
        return carry

    lax.fori_loop(0, num_chunks, step, 0)
    for c in range(num_chunks, num_chunks + max(-shift for _, shift, _ in order)):
        for name, shift, which in order:
            if shift < 0 and c + shift < num_chunks:
                if which is None:
                    acts[name](jnp.int32(c + shift))
                else:
                    guarded(which, acts[name], jnp.int32(c + shift))

    for c in range(num_chunks - SLOTS, num_chunks):
        c = jnp.int32(c)
        for k in range(2):
            for copy in p_copies(c, k) + [s_copy(c, k)]:
                copy.wait_send()

            @pl.when(jnp.logical_not(last))
            def _():
                for copy in y_copies(c, k, False):
                    copy.wait_send()

            @pl.when(turning)
            def _():
                c_copy(c, k).wait_send()

            @pl.when(last)
            def _():
                last_do(c, k, lambda copy: copy.wait_send(), lambda copy: copy.wait())
    for back in (2, 1):
        c = num_chunks - back * halves + y // per

        @pl.when(jnp.logical_not(jnp.logical_or(first, odd)))
        def _():
            wb_copy(c).wait_send()

    @pl.when(first)
    def _():
        for c in range(halves):
            @pl.when(owns(c))
            def _():
                for copy in x0_copies(jnp.int32(c)):
                    copy.wait_send()

    @pl.when(last)
    def _():
        for i in range(2):
            ref = gbuf.at[pl.ds(0, seqs - 1), pl.ds(0, seq_len - shard)]
            rcopy(ref, ref, g_send.at[i], g_send.at[i], others[0], stage).wait_send()
        for k in range(2):
            @pl.when(jnp.logical_or(per == 1, share(y, k) != lax.rem(y, per)))
            def _():
                arrived(out_ref.at[0, :, :, pl.ds(0, sb), col[k]], out_sem.at[k])

    @pl.when(jnp.logical_not(last))
    def _():
        arrived(out_ref.at[0], out_sem.at[0])


def solution(mesh):
    stages, rows = mesh.shape["pp"], mesh.shape["tp"]

    def stage_body(x_in, ln_params, w_q, w_k, w_v, w_o, w_up, w_down):
        num_micro, batch, shard, d_model = x_in.shape
        heads, hd = w_k.shape[2:]
        ff = w_up.shape[2]
        attn = heads * hd
        seq_len = shard * rows
        chunk = seq_len // HALVES
        num_chunks = num_micro * batch * HALVES
        sb = chunk // 2
        half = d_model // 2
        w_qkv = [w.reshape(d_model, attn) for w in (w_q, w_k, w_v)]
        cos_tab, sin_tab = rope_tables(seq_len, hd)
        dims = (stages, rows, batch, seq_len, chunk, d_model, heads, hd, ff)
        hbm = pl.BlockSpec(memory_space=pl.ANY)
        vmem = pl.BlockSpec(memory_space=pltpu.VMEM)
        dma = pltpu.SemaphoreType.DMA
        return pl.pallas_call(
            functools.partial(pipeline_kernel, dims),
            out_shape=(jax.ShapeDtypeStruct((1,) + x_in.shape, BF16), jax.ShapeDtypeStruct((num_micro * batch, seq_len, d_model), BF16)),
            in_specs=[hbm, vmem, vmem, vmem] + [hbm] * 6,
            out_specs=(hbm, hbm),
            scratch_shapes=[
                pltpu.VMEM((d_model, 3 * attn), BF16),
                pltpu.VMEM((d_model, ff), BF16),
                pltpu.VMEM((attn + ff, d_model), BF16),
                pltpu.VMEM((num_chunks, chunk, d_model), BF16),
                pltpu.VMEM((SLOTS, 2, sb, half), BF16),
                pltpu.VMEM((SLOTS, chunk, d_model), BF16),
                pltpu.VMEM((SLOTS, 2, sb, half), BF16),
                pltpu.VMEM((num_chunks, 2, sb, half), BF16),
                pltpu.VMEM((num_chunks, 2, sb, half), BF16),
                pltpu.VMEM((chunk, d_model), BF16),
                pltpu.VMEM((chunk, d_model), BF16),
                pltpu.VMEM((chunk, attn + ff), BF16),
                pltpu.VMEM((chunk, attn), BF16),
                pltpu.VMEM((seq_len, attn), BF16),
                pltpu.VMEM((seq_len, attn), BF16),
                dma((6,)),
                dma((num_chunks,)),
                dma((num_chunks, 2)),
                dma((num_chunks, 2)),
                dma((num_chunks, 2)),
                dma((2,)),
                dma((rows - 1,)),
                dma((num_micro * batch,)),
                dma((2,)),
                dma((2,)),
                dma((SLOTS, 2 * TILES)),
                dma((SLOTS, 2)),
                dma((SLOTS, 2, 2)),
                dma((SLOTS, 2)),
                dma((SLOTS, 2)),
            ],
            compiler_params=pltpu.CompilerParams(collective_id=0, has_side_effects=True, vmem_limit_bytes=67_000_000),
        )(x_in, ln_params[0], cos_tab, sin_tab, *w_qkv, w_o.reshape(attn, d_model), w_up[0], w_down[0])[0]

    in_specs = (P(None, "dp", "tp", None), P("pp", None, None), P("pp", None, "tp", None, None), P("pp", None, "tp", None), P("pp", None, "tp", None), P("pp", "tp", None, None, None), P("pp", None, "tp"), P("pp", "tp", None))
    return jax.shard_map(stage_body, mesh=mesh, in_specs=in_specs, out_specs=P("pp", None, "dp", "tp", None), check_vma=False)
```

time: 2440 us -> 380 us (0.16)
  waiting for transfers between devices: 1260 us -> 0 us
  matrix products: 799 us -> 0 us
  Pallas kernels: 0 us -> 370 us
  other arithmetic: 199 us -> 0 us
  local copies, waits for them, and re-layouts: 130 us -> 10.2 us
    dot_general x63 -> x0, matrix products: 799 us -> none  [the longest x9 373 us: branch_partial(): jnp.dot(h_mlp, w_up, preferred_element_type=jnp.float32)]
    all_gather x9 -> x0, waiting for transfers between devices: 686 us -> none  [stage_layer(): x_full = lax.all_gather(x_shard, 'tp', axis=1, tiled=True)]
    reduce_scatter x9 -> x0, waiting for transfers between devices: 537 us -> none  [stage_layer(): lax.psum_scatter(partial_sum, 'tp', scatter_dimension=1, tiled=True)]
    pallas_call x0 -> x1, Pallas kernels: none -> 370 us  [stage_body(): pl.pallas_call(functools.partial(pipeline_kernel, dims), out_shape=(jax.S...]
    while x290 -> x0, local copies, waits for them, and re-layouts: 72.2 us -> none
    convert_element_type x9 -> x0, other arithmetic: 52.7 us -> none  [layer_norm(): (centred * lax.rsqrt(variance + LN_EPS) * ln_gain + ln_bias).astype(jnp.b...]
    reduce_sum x18 -> x0, other arithmetic: 50.4 us -> none  [the longest x9 34.4 us: layer_norm(): row_mean = jnp.mean(x_f32, axis=-1, keepdims=True)]
    ppermute x9 -> x0, waiting for transfers between devices: 40 us -> none  [micro_step(): recv_buf = lax.ppermute(layer_out, 'pp', send_pairs)]
  transfers between devices with their start and end apart: 27 -> 0, of which waited for: 27 -> 0; matrix products, arithmetic and copies ran while one was open for 1% -> 0% of each run, Pallas kernels for 0% -> 0%
where the time goes in v2:
time: 380 us
  Pallas kernels  370 us (97%)
  local copies, waits for them, and re-layouts  10.2 us (3%)
    pallas_call x1, Pallas kernels, stage_body(): pl.pallas_call(functools.partial(pipeline_kernel, dims), out_shape=(jax.S...  370 us

profile of v2, /device:TPU:119, one launch (start us, length us, event | category | flops | bytes accessed | tf_op | source)
XLA Modules:
  0.0 379.8 jit_solution(16523140972180406699)
XLA Ops:
  0.0 0.0 copy-start
  0.0 0.0 copy-start.1
  0.0 3.4 copy.17
  3.4 0.0 copy-done
  3.4 0.0 copy-done.1
  3.4 2.8 copy_bitcast_fusion
  6.2 369.6 %shard_map.100 = (bf16[1,2,6,64,2048]{4,3,2,1,0:T(8,128)(2,1)}, bf16[12,256,2048]{2,1,0:T(8,128)(2,1)}) custom-call(bf16[2,6,64,2048]{3,2,1,0:T(8,128)(2,1)} %x_in.1, f32[4,2048]{1,0:T(4,128)} %bitcast.25, f32[256,128]{1,0:T(8,128)} %constant.4.clone.cos_ref, f32[256,128]{1,0:T(8,128)} %constant.5.clone.sin_ref, bf16[2048,512]{1,0:T(8,128)(2,1)} %bitcast.20, ...), custom_call_target="tpu_custom_call" | custom-call | tf_op jit(solution)/shard_map/pallas_call | solution.py:472
  375.8 4.0 %copy.19 = bf16[1,2,6,64,2048]{4,3,2,1,0:T(8,128)(2,1)} copy(bf16[1,2,6,64,2048]{4,3,2,1,0:T(8,128)(2,1)} %get-tuple-element.6) | data formatting | bytes 6291456
Async XLA Ops:
  0.0 3.4 copy-start
  0.0 3.4 copy-start.1

commit v3 on v2

--- a/solution.py
+++ b/solution.py
@@ -18,7 +18,7 @@
 HALVES = 2
 SLOTS = 2
 DIRECT = 8
-ORDER = ("W", "N", "Q", "s-1", "t-1", "Z", "x-2o", "y-2o", "a", "b", "F-1", "G-1")
+ORDER = ("W", "N", "s-1", "t-1", "Ye", "Zo", "ao", "x-2o", "y-2o", "b", "F-1", "G-1")
 LN_ROWS = 16
 
 
@@ -31,7 +31,7 @@
 
 
 def pipeline_kernel(dims, x_in, ln_par, cos_ref, sin_ref, wq_hbm, wk_hbm, wv_hbm, wo_hbm, wup_hbm, wdn_hbm, out_ref, gbuf,
-                    wqkv, wup, wod, xbuf, yst, pst, sst, rec1, rec2, ha, hm, act, qs, kc, vc,
+                    raw, wqkv, wup, wod, xbuf, yst, pst, sst, rec1, rec2, ha, hm, stat, act, qs, kc, vc,
                     w_sem, x_sem, one_sem, two_sem, cr_sem, out_sem, x0_send, g_sem, g_send, wb_send, p_send, s_send, y_send, l_send, c_send):
     stages, rows, batch, seq_len, chunk, d_model, heads, hd, ff = dims
     halves = seq_len // chunk
@@ -78,7 +78,7 @@
     def arrived(ref, sem):
         rcopy(ref, ref, sem, sem, others[0], stage).wait_recv()
 
-    places = [(src, wqkv.at[:, pl.ds(i * attn, attn)]) for i, src in enumerate((wq_hbm, wk_hbm, wv_hbm))]
+    places = [(src, raw.at[i]) for i, src in enumerate((wq_hbm, wk_hbm, wv_hbm))]
     places += [(wup_hbm, wup), (wo_hbm, wod.at[pl.ds(0, attn)]), (wdn_hbm, wod.at[pl.ds(attn, ff)])]
     weights = [pltpu.make_async_copy(src, dst, w_sem.at[i]) for i, (src, dst) in enumerate(places)]
     for copy in weights:
@@ -135,14 +135,16 @@
             out.append(rcopy(gbuf.at[sigma, rows_of(row)], xbuf.at[c, within(row)], g_send.at[1], x_sem.at[c], y, 0))
         return out
 
+    def x0_start(c):
+        @pl.when(owns(c))
+        def _():
+            for copy in x0_copies(jnp.int32(c)):
+                copy.start()
+
     def feed():
         @pl.when(first)
         def _():
-            for c in range(halves):
-                @pl.when(owns(c))
-                def _():
-                    for copy in x0_copies(jnp.int32(c)):
-                        copy.start()
+            x0_start(0)
             for c in range(num_chunks):
                 @pl.when(owns(c))
                 def _():
@@ -153,6 +155,10 @@
             for sigma in range(1, seqs):
                 for copy in g_exchange(sigma):
                     copy.start()
+
+    def pass_on():
+        @pl.when(last)
+        def _():
             for sigma in range(1, seqs):
                 arrived(gbuf.at[sigma, pl.ds(0, seq_len - shard)], g_sem.at[sigma])
                 for copy in g_pass(sigma):
@@ -172,35 +178,36 @@
                 wb_copy(c - 2 * halves).wait_send()
             wb_copy(c).start()
 
-    def p_copies(c, k):
-        p = lax.rem(c, SLOTS)
-        out = []
-        for i in range(TILES):
-            cols = pl.ds(k * half + i * tile, tile)
-            out.append(rcopy(pst.at[p, tokens(share(cross[k], k)), cols], rec1.at[c, k, :, pl.ds(i * tile, tile)],
-                             p_send.at[p, k * TILES + i], one_sem.at[c, k], cross[k], stage))
-        return out
-
-    def s_copy(c, k):
-        p = lax.rem(c, SLOTS)
-        return rcopy(sst.at[p, k], rec2.at[c, k], s_send.at[p, k], two_sem.at[c, k], partner[k], stage)
+    def piece(k, i):
+        return pl.ds(k * half + i * tile, tile)
+
+    def p_copy(c, k, i):
+        p = lax.rem(c, SLOTS)
+        return rcopy(pst.at[p, tokens(share(cross[k], k)), piece(k, i)], rec1.at[c, k, :, piece(0, i)],
+                     p_send.at[p, k, i], one_sem.at[c, k], cross[k], stage)
+
+    def s_copy(c, k, i):
+        p = lax.rem(c, SLOTS)
+        return rcopy(sst.at[p, k, :, piece(0, i)], rec2.at[c, k, :, piece(0, i)], s_send.at[p, k, i], two_sem.at[c, k, i], partner[k], stage)
 
     def first_sum(c, k):
         p = lax.rem(c, SLOTS)
 
         @pl.when(c >= SLOTS)
         def _():
-            s_copy(c - SLOTS, k).wait_send()
+            for i in range(TILES):
+                s_copy(c - SLOTS, k, i).wait_send()
         arrived(rec1.at[c, k], one_sem.at[c, k])
         own = pst[p, tokens(share(y, k)), col[k]]
         sst[p, k] = (rec1[c, k].astype(F32) + own.astype(F32)).astype(BF16)
-        s_copy(c, k).start()
-
-    def y_copies(c, k, around):
-        p = lax.rem(c, SLOTS)
-        where = (c, tokens(share(y, k)), col[k])
-        side = rcopy(yst.at[p, k], xbuf.at[where], y_send.at[p, k, 0], cr_sem.at[c, k] if around else x_sem.at[c], cross[k], stage if around else nxt)
-        return [side, rcopy(yst.at[p, k], xbuf.at[where], y_send.at[p, k, 1], x_sem.at[c], y, nxt)]
+        for i in range(TILES):
+            s_copy(c, k, i).start()
+
+    def y_copies(c, k, i, around):
+        p = lax.rem(c, SLOTS)
+        src, where = yst.at[p, k, :, piece(0, i)], (c, tokens(share(y, k)), piece(k, i))
+        side = rcopy(src, xbuf.at[where], y_send.at[p, k, i, 0], cr_sem.at[c, k] if around else x_sem.at[c], cross[k], stage if around else nxt)
+        return [side, rcopy(src, xbuf.at[where], y_send.at[p, k, i, 1], x_sem.at[c], y, nxt)]
 
     def c_copy(c, k):
         ref = xbuf.at[c, tokens(share(cross[k], k)), col[k]]
@@ -215,66 +222,76 @@
             arrived(xbuf.at[c, tokens(share(cross[k], k)), col[k]], cr_sem.at[c, k])
             c_copy(c, k).start()
 
-    def last_place(c, k):
+    def last_place(c, k, i):
         token = lax.rem(c, halves) * chunk + share(y, k) * sb
         start = pl.multiple_of(lax.rem(token, shard), sb)
         m, b = seq_of(c)
-        return token // shard, out_ref.at[0, m, b, pl.ds(start, sb), col[k]]
-
-    def last_do(c, k, remote, local):
-        p = lax.rem(c, SLOTS)
-        row, dst = last_place(c, k)
+        return token // shard, out_ref.at[0, m, b, pl.ds(start, sb), piece(k, i)]
+
+    def last_do(c, k, i, remote, local):
+        p = lax.rem(c, SLOTS)
+        row, dst = last_place(c, k, i)
+        src, sem = yst.at[p, k, :, piece(0, i)], l_send.at[p, k, i]
 
         @pl.when(row == cross[k])
         def _():
-            remote(rcopy(yst.at[p, k], dst, l_send.at[p, k], out_sem.at[k], cross[k], stage))
+            remote(rcopy(src, dst, sem, out_sem.at[k], cross[k], stage))
 
         @pl.when(row == y)
         def _():
-            local(pltpu.make_async_copy(yst.at[p, k], dst, l_send.at[p, k]))
-
-    def finish_half(c, k):
-        p = lax.rem(c, SLOTS)
-
-        @pl.when(jnp.logical_and(c >= SLOTS, jnp.logical_not(last)))
-        def _():
-            for copy in y_copies(c - SLOTS, k, False):
-                copy.wait_send()
-
-        @pl.when(jnp.logical_and(c >= SLOTS, last))
-        def _():
-            last_do(c - SLOTS, k, lambda copy: copy.wait_send(), lambda copy: copy.wait())
-        arrived(rec2.at[c, k], two_sem.at[c, k])
-        total = sst[p, k].astype(F32) + rec2[c, k].astype(F32)
-        yst[p, k] = (xbuf[c, tokens(share(y, k)), col[k]].astype(F32) + total).astype(BF16)
-
+            local(pltpu.make_async_copy(src, dst, sem))
+
+    def finish(c, i):
+        p = lax.rem(c, SLOTS)
         around = jnp.logical_and(turning, c >= DIRECT)
-
-        @pl.when(around)
-        def _():
-            for copy in y_copies(c, k, True):
-                copy.start()
-
-        @pl.when(jnp.logical_not(jnp.logical_or(around, last)))
-        def _():
-            for copy in y_copies(c, k, False):
-                copy.start()
-
-        @pl.when(last)
-        def _():
-            last_do(c, k, lambda copy: copy.start(), lambda copy: copy.start())
+        for k in range(2):
+            @pl.when(jnp.logical_and(c >= SLOTS, jnp.logical_not(last)))
+            def _():
+                for copy in y_copies(c - SLOTS, k, i, False):
+                    copy.wait_send()
+
+            @pl.when(jnp.logical_and(c >= SLOTS, last))
+            def _():
+                last_do(c - SLOTS, k, i, lambda copy: copy.wait_send(), lambda copy: copy.wait())
+            arrived(rec2.at[c, k, :, piece(0, i)], two_sem.at[c, k, i])
+            total = sst[p, k, :, piece(0, i)].astype(F32) + rec2[c, k, :, piece(0, i)].astype(F32)
+            yst[p, k, :, piece(0, i)] = (xbuf[c, tokens(share(y, k)), piece(k, i)].astype(F32) + total).astype(BF16)
+
+            @pl.when(around)
+            def _():
+                for copy in y_copies(c, k, i, True):
+                    copy.start()
+
+            @pl.when(jnp.logical_not(jnp.logical_or(around, last)))
+            def _():
+                for copy in y_copies(c, k, i, False):
+                    copy.start()
+
+            @pl.when(last)
+            def _():
+                last_do(c, k, i, lambda copy: copy.start(), lambda copy: copy.start())
+
+    lanes = stat.shape[2]
 
     def norms(c):
-        gain_a, bias_a = ln_par[0:1, :], ln_par[1:2, :]
-        gain_m, bias_m = ln_par[2:3, :], ln_par[3:4, :]
+        gain, bias = ln_par[0:1, :], ln_par[1:2, :]
         for start in range(0, chunk, LN_ROWS):
             part = pl.ds(start, LN_ROWS)
             x = xbuf[c, part].astype(F32)
-            centred = x - jnp.mean(x, axis=-1, keepdims=True)
+            mean = jnp.mean(x, axis=-1, keepdims=True)
+            centred = x - mean
             scale = lax.rsqrt(jnp.mean(centred * centred, axis=-1, keepdims=True) + LN_EPS)
-            normed = centred * scale
-            ha[part] = (normed * gain_a + bias_a).astype(BF16)
-            hm[part] = (normed * gain_m + bias_m).astype(BF16)
+            ha[part] = (centred * scale * gain + bias).astype(BF16)
+            stat[0, part] = jnp.broadcast_to(mean, (LN_ROWS, lanes))
+            stat[1, part] = jnp.broadcast_to(scale, (LN_ROWS, lanes))
+
+    def second_norms(c, begin, end):
+        for start in range(begin, end, LN_ROWS):
+            part = pl.ds(start, LN_ROWS)
+            mean, scale = stat[0, part], stat[1, part]
+            for left in range(0, d_model, lanes):
+                cols = slice(left, left + lanes)
+                hm[part, cols] = ((xbuf[c, part, cols].astype(F32) - mean) * scale * ln_par[2:3, cols] + ln_par[3:4, cols]).astype(BF16)
 
     def project(c):
         start = pl.multiple_of(lax.rem(c, halves) * chunk, chunk)
@@ -289,9 +306,11 @@
         q = jnp.dot(h, wqkv[:, 0:attn], preferred_element_type=F32)
         for i in range(heads):
             qs[:, i * hd:(i + 1) * hd] = rope(q[:, i * hd:(i + 1) * hd])
+        second_norms(c, 0, chunk // 2)
         k = jnp.dot(h, wqkv[:, attn:2 * attn], preferred_element_type=F32)
         for i in range(heads):
             kc[where, i * hd:(i + 1) * hd] = rope(k[:, i * hd:(i + 1) * hd])
+        second_norms(c, chunk // 2, chunk)
         vc[where, :] = jnp.dot(h, wqkv[:, 2 * attn:3 * attn], preferred_element_type=F32).astype(BF16)
 
     def attend(c, i):
@@ -307,18 +326,10 @@
         cols = slice(i * hd, (i + 1) * hd)
         act[:, cols] = jnp.dot(probs, vc[:, cols], preferred_element_type=F32).astype(BF16)
 
-    def attention(c):
-        for i in range(heads):
-            contract(i, attend(c, i))
-
     def up_tile(i, width):
         cols = slice(i * width, (i + 1) * width)
         u = jnp.dot(hm[...], wup[:, cols], preferred_element_type=F32)
         act[:, attn + i * width:attn + (i + 1) * width] = (0.5 * u * (1.0 + lax.erf(u * np.float32(0.5 ** 0.5)))).astype(BF16)
-
-    def mlp_up():
-        for i in range(ff // COL_TILE):
-            up_tile(i, COL_TILE)
 
     def attention_and_up(c):
         for i in range(heads):
@@ -326,54 +337,71 @@
             up_tile(i, ff // heads)
             contract(i, probs)
 
-    def down(c, k):
+    def down(c, i):
         p = lax.rem(c, SLOTS)
         a = act[...]
-        copies = p_copies(c, k)
-        for i, start in enumerate(range(k * half, (k + 1) * half, tile)):
-            cols = slice(start, start + tile)
-            out = jnp.dot(a, wod[:, cols], preferred_element_type=F32)
-            pst[p, :, cols] = out.astype(BF16)
-            copies[i].start()
+        for k in range(2):
+            cols = slice(k * half + i * tile, k * half + (i + 1) * tile)
+            pst[p, :, cols] = jnp.dot(a, wod[:, cols], preferred_element_type=F32).astype(BF16)
+        for k in range(2):
+            p_copy(c, k, i).start()
 
     kc[...] = jnp.zeros_like(kc)
     vc[...] = jnp.zeros_like(vc)
     feed()
 
-    def loaded(c, which):
-        @pl.when(c == 0)
-        def _():
-            for copy in which:
-                copy.wait()
-
-    def project_first(c):
-        loaded(c, weights[:3])
+    depth = hd // 2
+    group = depth * heads
+    out_row, in_row = (lax.broadcasted_iota(jnp.int32, (group, group), axis) for axis in (0, 1))
+    pick = (in_row == heads * lax.rem(out_row, depth) + out_row // depth).astype(F32).astype(BF16)
+    for copy in weights[:3]:
+        copy.wait()
+
+    def sort_heads(j, carry):
+        rows_in = pl.ds(pl.multiple_of(j * group, group), group)
+        rows_out = pl.ds(pl.multiple_of(j * depth, depth), depth)
+        pair = jnp.dot(pick, jnp.concatenate([raw[0, rows_in], raw[1, rows_in]], axis=1), preferred_element_type=F32).astype(BF16)
+        alone = jnp.dot(pick, raw[2, rows_in], preferred_element_type=F32).astype(BF16)
+        for i, val in enumerate((pair[:, :hd], pair[:, hd:], alone)):
+            for h in range(heads):
+                wqkv[rows_out, i * attn + h * hd:i * attn + (h + 1) * hd] = val[h * depth:(h + 1) * depth]
+        return carry
+
+    lax.fori_loop(0, d_model // depth, sort_heads, 0, unroll=4)
+    @pl.when(first)
+    def _():
+        for c in range(1, halves):
+            x0_start(c)
+    pass_on()
+    for copy in weights[3:]:
+        copy.wait()
+
+    def free_sums(c):
+        @pl.when(c >= SLOTS)
+        def _():
+            for k in range(2):
+                for i in range(TILES):
+                    p_copy(c - SLOTS, k, i).wait_send()
+
+        @pl.when(jnp.logical_and(odd, owns(c)))
+        def _():
+            wb_copy(c).wait_send()
+
+    def down_a(c):
+        free_sums(c)
+        down(c, 0)
+
+    def middle(c):
+        free_sums(c)
+        attention_and_up(c)
+        down(c, 0)
+
+    def norms_and_project(c):
+        norms(c)
         project(c)
 
-    def mlp_up_first(c):
-        loaded(c, weights[3:4])
-        mlp_up()
-
-    def both(c):
-        loaded(c, weights[3:4])
-        attention_and_up(c)
-
-    def down_a(c):
-        loaded(c, weights[4:])
-
-        @pl.when(c >= SLOTS)
-        def _():
-            for k in range(2):
-                for copy in p_copies(c - SLOTS, k):
-                    copy.wait_send()
-
-        @pl.when(jnp.logical_and(odd, owns(c)))
-        def _():
-            wb_copy(c).wait_send()
-        down(c, 0)
-
-    acts = {"W": wait_x, "N": norms, "Q": project_first, "A": attention, "U": mlp_up_first, "Z": both, "a": down_a, "b": lambda c: down(c, 1),
-            "s": lambda c: first_sum(c, 0), "t": lambda c: first_sum(c, 1), "x": lambda c: carry(c, 0), "y": lambda c: carry(c, 1), "F": lambda c: finish_half(c, 0), "G": lambda c: finish_half(c, 1)}
+    acts = {"W": wait_x, "N": norms_and_project, "Z": attention_and_up, "Y": middle, "a": down_a, "b": lambda c: down(c, 1),
+            "s": lambda c: first_sum(c, 0), "t": lambda c: first_sum(c, 1), "x": lambda c: carry(c, 0), "y": lambda c: carry(c, 1), "F": lambda c: finish(c, 0), "G": lambda c: finish(c, 1)}
     order = [(o[0], int(o[1:].rstrip("eo") or 0), {"e": jnp.logical_not(odd), "o": odd}.get(o[-1])) for o in ORDER]
 
     def guarded(ok, fn, c):
@@ -405,21 +433,22 @@
     for c in range(num_chunks - SLOTS, num_chunks):
         c = jnp.int32(c)
         for k in range(2):
-            for copy in p_copies(c, k) + [s_copy(c, k)]:
-                copy.wait_send()
-
-            @pl.when(jnp.logical_not(last))
-            def _():
-                for copy in y_copies(c, k, False):
-                    copy.wait_send()
+            for i in range(TILES):
+                p_copy(c, k, i).wait_send()
+                s_copy(c, k, i).wait_send()
+
+                @pl.when(jnp.logical_not(last))
+                def _():
+                    for copy in y_copies(c, k, i, False):
+                        copy.wait_send()
+
+                @pl.when(last)
+                def _():
+                    last_do(c, k, i, lambda copy: copy.wait_send(), lambda copy: copy.wait())
 
             @pl.when(turning)
             def _():
                 c_copy(c, k).wait_send()
-
-            @pl.when(last)
-            def _():
-                last_do(c, k, lambda copy: copy.wait_send(), lambda copy: copy.wait())
     for back in (2, 1):
         c = num_chunks - back * halves + y // per
 
@@ -448,6 +477,19 @@
     @pl.when(jnp.logical_not(last))
     def _():
         arrived(out_ref.at[0], out_sem.at[0])
+
+
+def copy_kernel(src, dst, held, sems):
+    places = [(m, b) for m in range(held.shape[0]) for b in range(held.shape[1])]
+    into = [pltpu.make_async_copy(src.at[0, m, b], held.at[m, b], sems.at[0, m, b]) for m, b in places]
+    out_of = [pltpu.make_async_copy(held.at[m, b], dst.at[0, m, b], sems.at[1, m, b]) for m, b in places]
+    for copy in into:
+        copy.start()
+    for first, second in zip(into, out_of):
+        first.wait()
+        second.start()
+    for copy in out_of:
+        copy.wait()
 
 
 def solution(mesh):
@@ -463,18 +505,19 @@
         num_chunks = num_micro * batch * HALVES
         sb = chunk // 2
         half = d_model // 2
-        w_qkv = [w.reshape(d_model, attn) for w in (w_q, w_k, w_v)]
+        w_qkv = [w.reshape(d_model * heads, hd) for w in (w_q, w_k, w_v)]
         cos_tab, sin_tab = rope_tables(seq_len, hd)
         dims = (stages, rows, batch, seq_len, chunk, d_model, heads, hd, ff)
         hbm = pl.BlockSpec(memory_space=pl.ANY)
         vmem = pl.BlockSpec(memory_space=pltpu.VMEM)
         dma = pltpu.SemaphoreType.DMA
-        return pl.pallas_call(
+        out = pl.pallas_call(
             functools.partial(pipeline_kernel, dims),
             out_shape=(jax.ShapeDtypeStruct((1,) + x_in.shape, BF16), jax.ShapeDtypeStruct((num_micro * batch, seq_len, d_model), BF16)),
             in_specs=[hbm, vmem, vmem, vmem] + [hbm] * 6,
             out_specs=(hbm, hbm),
             scratch_shapes=[
+                pltpu.VMEM((3, d_model * heads, hd), BF16),
                 pltpu.VMEM((d_model, 3 * attn), BF16),
                 pltpu.VMEM((d_model, ff), BF16),
                 pltpu.VMEM((attn + ff, d_model), BF16),
@@ -486,6 +529,7 @@
                 pltpu.VMEM((num_chunks, 2, sb, half), BF16),
                 pltpu.VMEM((chunk, d_model), BF16),
                 pltpu.VMEM((chunk, d_model), BF16),
+                pltpu.VMEM((2, chunk, hd), F32),
                 pltpu.VMEM((chunk, attn + ff), BF16),
                 pltpu.VMEM((chunk, attn), BF16),
                 pltpu.VMEM((seq_len, attn), BF16),
@@ -493,21 +537,24 @@
                 dma((6,)),
                 dma((num_chunks,)),
                 dma((num_chunks, 2)),
-                dma((num_chunks, 2)),
+                dma((num_chunks, 2, TILES)),
                 dma((num_chunks, 2)),
                 dma((2,)),
                 dma((rows - 1,)),
                 dma((num_micro * batch,)),
                 dma((2,)),
                 dma((2,)),
-                dma((SLOTS, 2 * TILES)),
-                dma((SLOTS, 2)),
-                dma((SLOTS, 2, 2)),
-                dma((SLOTS, 2)),
+                dma((SLOTS, 2, TILES)),
+                dma((SLOTS, 2, TILES)),
+                dma((SLOTS, 2, TILES, 2)),
+                dma((SLOTS, 2, TILES)),
                 dma((SLOTS, 2)),
             ],
             compiler_params=pltpu.CompilerParams(collective_id=0, has_side_effects=True, vmem_limit_bytes=67_000_000),
         )(x_in, ln_params[0], cos_tab, sin_tab, *w_qkv, w_o.reshape(attn, d_model), w_up[0], w_down[0])[0]
+        return pl.pallas_call(
+            copy_kernel, in_specs=[hbm], out_specs=hbm, out_shape=jax.ShapeDtypeStruct(out.shape, out.dtype),
+            scratch_shapes=[pltpu.VMEM(out.shape[1:], BF16), dma((2, num_micro, batch))])(out)
 
     in_specs = (P(None, "dp", "tp", None), P("pp", None, None), P("pp", None, "tp", None, None), P("pp", None, "tp", None), P("pp", None, "tp", None), P("pp", "tp", None, None, None), P("pp", None, "tp"), P("pp", "tp", None))
     return jax.shard_map(stage_body, mesh=mesh, in_specs=in_specs, out_specs=P("pp", None, "dp", "tp", None), check_vma=False)

time: 380 us -> 369 us (0.971)
  local copies, waits for them, and re-layouts: 10.2 us -> 0 us
    unnamed x6 -> x0, local copies, waits for them, and re-layouts: 7.4 us -> none
where the time goes in v3:
time: 369 us
  Pallas kernels  369 us (100%)
    pallas_call x1, Pallas kernels, stage_body(): pl.pallas_call(functools.partial(pipeline_kernel, dims), out_shape=(jax.S...  366 us

profile of v3, /device:TPU:119, one launch (start us, length us, event | category | flops | bytes accessed | tf_op | source)
XLA Modules:
  0.0 369.1 jit_solution(10692563432892807977)
XLA Ops:
  0.0 366.3 %shard_map.100 = (bf16[1,2,6,64,2048]{4,3,2,1,0:T(8,128)(2,1)}, bf16[12,256,2048]{2,1,0:T(8,128)(2,1)}) custom-call(bf16[2,6,64,2048]{3,2,1,0:T(8,128)(2,1)} %x_in.1, f32[4,2048]{1,0:T(4,128)} %bitcast.13, f32[256,128]{1,0:T(8,128)} %constant.4.clone.cos_ref, f32[256,128]{1,0:T(8,128)} %constant.5.clone.sin_ref, bf16[8192,128]{1,0:T(8,128)(2,1)} %bitcast.9, ...), custom_call_target="tpu_custom_call" | custom-call | tf_op jit(solution)/shard_map/pallas_call | solution.py:514
  366.3 2.8 shard_map.101

commit v4 on v3

--- a/solution.py
+++ b/solution.py
@@ -18,7 +18,8 @@
 HALVES = 2
 SLOTS = 2
 DIRECT = 8
-ORDER = ("W", "N", "s-1", "t-1", "Ye", "Zo", "ao", "x-2o", "y-2o", "b", "F-1", "G-1")
+STEP = 0
+ORDER = ("W", "N", "s-1", "t-1", "Ye", "Zo", "x-2o", "ao", "y-2o", "b", "F-1", "G-1")
 LN_ROWS = 16
 
 
@@ -50,9 +51,10 @@
     last = stage == stages - 1
     nxt = jnp.minimum(stage + 1, stages - 1)
     prv = jnp.maximum(stage - 1, 0)
-    others = [lax.rem(y + shift, rows) for shift in range(1, rows)]
+    others = [lax.rem(y + shift, rows) for shift in sorted(range(1, rows), key=lambda n: min(n, rows - n))]
     odd = lax.rem(stage, 2) == 1
     turning = jnp.logical_and(odd, jnp.logical_not(last))
+    direct = DIRECT + STEP * (stage // 2)
 
     flip, mirror = y + 1 - 2 * lax.rem(y, 2), rows - 1 - y
     partner, cross = (flip, mirror), (mirror, flip)
@@ -206,21 +208,22 @@
     def y_copies(c, k, i, around):
         p = lax.rem(c, SLOTS)
         src, where = yst.at[p, k, :, piece(0, i)], (c, tokens(share(y, k)), piece(k, i))
-        side = rcopy(src, xbuf.at[where], y_send.at[p, k, i, 0], cr_sem.at[c, k] if around else x_sem.at[c], cross[k], stage if around else nxt)
+        side = rcopy(src, xbuf.at[where], y_send.at[p, k, i, 0], cr_sem.at[c, k, i] if around else x_sem.at[c], cross[k], stage if around else nxt)
         return [side, rcopy(src, xbuf.at[where], y_send.at[p, k, i, 1], x_sem.at[c], y, nxt)]
 
-    def c_copy(c, k):
-        ref = xbuf.at[c, tokens(share(cross[k], k)), col[k]]
-        return rcopy(ref, ref, c_send.at[lax.rem(c, SLOTS), k], x_sem.at[c], y, nxt)
-
-    def carry(c, k):
-        @pl.when(jnp.logical_and(turning, c >= DIRECT))
-        def _():
-            @pl.when(c >= DIRECT + SLOTS)
-            def _():
-                c_copy(c - SLOTS, k).wait_send()
-            arrived(xbuf.at[c, tokens(share(cross[k], k)), col[k]], cr_sem.at[c, k])
-            c_copy(c, k).start()
+    def c_copy(c, k, i):
+        ref = xbuf.at[c, tokens(share(cross[k], k)), piece(k, i)]
+        return rcopy(ref, ref, c_send.at[lax.rem(c, SLOTS), k, i], x_sem.at[c], y, nxt)
+
+    def carry(c, i):
+        @pl.when(jnp.logical_and(turning, c >= direct))
+        def _():
+            for k in range(2):
+                @pl.when(c >= direct + SLOTS)
+                def _():
+                    c_copy(c - SLOTS, k, i).wait_send()
+                arrived(xbuf.at[c, tokens(share(cross[k], k)), piece(k, i)], cr_sem.at[c, k, i])
+                c_copy(c, k, i).start()
 
     def last_place(c, k, i):
         token = lax.rem(c, halves) * chunk + share(y, k) * sb
@@ -243,7 +246,7 @@
 
     def finish(c, i):
         p = lax.rem(c, SLOTS)
-        around = jnp.logical_and(turning, c >= DIRECT)
+        around = jnp.logical_and(turning, c >= direct)
         for k in range(2):
             @pl.when(jnp.logical_and(c >= SLOTS, jnp.logical_not(last)))
             def _():
@@ -448,7 +451,8 @@
 
             @pl.when(turning)
             def _():
-                c_copy(c, k).wait_send()
+                for i in range(TILES):
+                    c_copy(c, k, i).wait_send()
     for back in (2, 1):
         c = num_chunks - back * halves + y // per
 
@@ -538,7 +542,7 @@
                 dma((num_chunks,)),
                 dma((num_chunks, 2)),
                 dma((num_chunks, 2, TILES)),
-                dma((num_chunks, 2)),
+                dma((num_chunks, 2, TILES)),
                 dma((2,)),
                 dma((rows - 1,)),
                 dma((num_micro * batch,)),
@@ -548,7 +552,7 @@
                 dma((SLOTS, 2, TILES)),
                 dma((SLOTS, 2, TILES, 2)),
                 dma((SLOTS, 2, TILES)),
-                dma((SLOTS, 2)),
+                dma((SLOTS, 2, TILES)),
             ],
             compiler_params=pltpu.CompilerParams(collective_id=0, has_side_effects=True, vmem_limit_bytes=67_000_000),
         )(x_in, ln_params[0], cos_tab, sin_tab, *w_qkv, w_o.reshape(attn, d_model), w_up[0], w_down[0])[0]

time: 369 us -> 368 us (level)
  no operation moved by 1% of the time
where the time goes in v4:
time: 368 us
  Pallas kernels  368 us (100%)
    pallas_call x1, Pallas kernels, stage_body(): pl.pallas_call(functools.partial(pipeline_kernel, dims), out_shape=(jax.S...  365 us

profile of v4, /device:TPU:119, one launch (start us, length us, event | category | flops | bytes accessed | tf_op | source)
XLA Modules:
  0.0 367.9 jit_solution(5653045769600013323)
XLA Ops:
  0.0 365.1 %shard_map.100 = (bf16[1,2,6,64,2048]{4,3,2,1,0:T(8,128)(2,1)}, bf16[12,256,2048]{2,1,0:T(8,128)(2,1)}) custom-call(bf16[2,6,64,2048]{3,2,1,0:T(8,128)(2,1)} %x_in.1, f32[4,2048]{1,0:T(4,128)} %bitcast.13, f32[256,128]{1,0:T(8,128)} %constant.4.clone.cos_ref, f32[256,128]{1,0:T(8,128)} %constant.5.clone.sin_ref, bf16[8192,128]{1,0:T(8,128)(2,1)} %bitcast.9, ...), custom_call_target="tpu_custom_call" | custom-call | tf_op jit(solution)/shard_map/pallas_call | solution.py:518
  365.1 2.8 shard_map.101

commit v5 on v4

--- a/solution.py
+++ b/solution.py
@@ -84,7 +84,7 @@
     places += [(wup_hbm, wup), (wo_hbm, wod.at[pl.ds(0, attn)]), (wdn_hbm, wod.at[pl.ds(attn, ff)])]
     weights = [pltpu.make_async_copy(src, dst, w_sem.at[i]) for i, (src, dst) in enumerate(places)]
     for copy in weights:
-        copy.start()
+        copy.start(priority=1)
 
     barrier = pltpu.get_barrier_semaphore()
     for row in others:

time: 368 us -> 368 us (level)
  no operation moved by 1% of the time
where the time goes in v5:
time: 368 us
  Pallas kernels  368 us (100%)
    pallas_call x1, Pallas kernels, stage_body(): pl.pallas_call(functools.partial(pipeline_kernel, dims), out_shape=(jax.S...  365 us

profile of v5, /device:TPU:119, one launch (start us, length us, event | category | flops | bytes accessed | tf_op | source)
XLA Modules:
  0.0 367.9 jit_solution(14395814816294858543)
XLA Ops:
  0.0 365.1 %shard_map.100 = (bf16[1,2,6,64,2048]{4,3,2,1,0:T(8,128)(2,1)}, bf16[12,256,2048]{2,1,0:T(8,128)(2,1)}) custom-call(bf16[2,6,64,2048]{3,2,1,0:T(8,128)(2,1)} %x_in.1, f32[4,2048]{1,0:T(4,128)} %bitcast.13, f32[256,128]{1,0:T(8,128)} %constant.4.clone.cos_ref, f32[256,128]{1,0:T(8,128)} %constant.5.clone.sin_ref, bf16[8192,128]{1,0:T(8,128)(2,1)} %bitcast.9, ...), custom_call_target="tpu_custom_call" | custom-call | tf_op jit(solution)/shard_map/pallas_call | solution.py:518
  365.1 2.8 shard_map.101
